TPU v7x, 32 devices: a whole 2x2x4 slice. The times are simulated.
32 devices in a mesh: aux: 8 (over z, x), lmo: 4 (over y, core).
Axes of the slice: x: 2, y: 2, z: 4, core: 2. Of those that a mesh axis runs over, the one named last changes fastest.
Arguments:
- aux_ints: bfloat16 [256, 768, 768], P(('aux', 'lmo')), may hold values from -6 to 6
- lmo_coef: bfloat16 [128, 384], P(('aux', 'lmo')), may hold values from -0.3125 to 0.3125
- ao_domain: int32 [128, 3], replicated, may hold values from 0 to 5, as said below
- ao_count: int32 [128], replicated, may hold values from 1 to 3
- pao_domain: int32 [128, 3], replicated, may hold values from 0 to 5, as said below
- pao_count: int32 [128], replicated, may hold values from 1 to 3, as said below
- owner_order: int32 [128], replicated, may hold values from 0 to 127, as said below
- pao_coef: bfloat16 [128, 384, 256], P(('aux', 'lmo')), may hold values from -0.3125 to 0.3125
Outputs:
- pair_ints: bfloat16 [128, 256, 256], P(('aux', 'lmo'))
- pair_metric: float32 [128, 256, 256], P(('aux', 'lmo'))
Inputs may be any that keep to these rules, and one draw needn't show every extreme that they name: `ao_domain`: each row holds 3 different block numbers; slots from ao_count on are unused. `pao_domain`: each row holds 3 different block numbers; slots from pao_count on are unused. `pao_count`: the LMOs of the 4 owner slots of one device use together at most 8 PAO block slots, and those of some device use exactly 8. `owner_order`: every LMO stands in exactly one slot.
All inputs are finite; a program needn't handle non-finite values.
Results may differ from a plain program's by a relative error of at most 0.0049.
Values may be sent and summed in bfloat16 or wider, within the bound.
No kernel may reach another device: no remote copies, remote signals or barrier semaphores. Data moves between devices by JAX's collectives and lax.ppermute only.
A program may use at most 128 MiB of HBM per device.

v0:
```python
import jax
import jax.numpy as jnp
from jax import lax
from jax.sharding import PartitionSpec as P

BLK = 128
DB = 3
PB = 3


def place(lmo_coef, domain, block_count, blocks):
    lmo_total = lmo_coef.shape[0]
    in_domain = jnp.arange(DB)[None, :] < block_count[:, None]
    onehot = (
        (domain[:, :, None] == jnp.arange(blocks)[None, None, :]) & in_domain[:, :, None]
    ).astype(jnp.float32)
    tiles = lmo_coef.astype(jnp.float32).reshape(lmo_total, DB, BLK)
    dense_coef = jnp.einsum("ikb,ikn->bni", onehot, tiles, precision=lax.Precision.HIGHEST)
    return dense_coef.reshape(blocks * BLK, lmo_total).astype(jnp.bfloat16)


def select(half_ints, domain, block_count, blocks):
    row_total = half_ints.shape[0]
    lmo_total = half_ints.shape[2]
    in_domain = jnp.arange(PB)[None, :] < block_count[:, None]
    onehot = (
        (domain[:, :, None] == jnp.arange(blocks)[None, None, :]) & in_domain[:, :, None]
    ).astype(jnp.float32)
    tiled = half_ints.reshape(row_total, blocks, BLK, lmo_total)
    picked = jnp.einsum("pbni,ikb->ipkn", tiled, onehot, precision=lax.Precision.HIGHEST)
    return picked.reshape(lmo_total, row_total, PB * BLK).astype(jnp.bfloat16)


def shards(aux_ints, lmo_coef, ao_domain, ao_count, pao_domain, pao_count, owner_order, pao_coef):
    all_coef = lax.all_gather(lmo_coef, ("aux", "lmo"), axis=0, tiled=True)
    row_total, ao_total, _ = aux_ints.shape
    blocks = ao_total // BLK
    dense_coef = place(all_coef, ao_domain, ao_count, blocks)
    half_ints = jnp.dot(
        aux_ints.reshape(row_total * ao_total, ao_total),
        dense_coef,
        preferred_element_type=jnp.float32,
    ).reshape(row_total, ao_total, -1)
    selected = select(half_ints, pao_domain, pao_count, blocks)
    ordered = jnp.take(selected, owner_order, axis=0)
    received = lax.all_to_all(ordered, ("aux", "lmo"), split_axis=0, concat_axis=1, tiled=True)
    aux_total = received.shape[1]
    pair_ints = jnp.einsum(
        "rpm,rma->rpa", received, pao_coef, preferred_element_type=jnp.float32
    ).astype(jnp.bfloat16)
    pair_metric = (
        jnp.einsum("rpa,rpb->rab", pair_ints, pair_ints, preferred_element_type=jnp.float32)
        / aux_total
    )
    return (pair_ints, pair_metric)


def solution(mesh):
    placed = (
        P(("aux", "lmo"), None, None),
        P(("aux", "lmo"), None),
        P(),
        P(),
        P(),
        P(),
        P(),
        P(("aux", "lmo"), None, None),
    )
    return jax.shard_map(
        shards,
        mesh=mesh,
        in_specs=placed,
        out_specs=(P(("aux", "lmo"), None, None), P(("aux", "lmo"), None, None)),
        check_vma=False,
    )
```

profile of v0, /device:TPU:5, one launch (start us, length us, event | category | flops | bytes accessed | tf_op | source)
XLA Modules:
  0.0 94.9 jit_solution(15737107026913845663)
XLA Ops:
  0.6 0.0 copy-start
  0.6 0.7 compare_select_fusion
  1.4 0.7 compare_and_fusion
  2.0 38.1 %all-gather = bf16[32,4,384]{2,1,0:T(4,128)(2,1)S(1)} all-gather(bf16[1,4,384]{2,1,0:T(4,128)(2,1)} %bitcast.32), channel_id=1, replica_groups=mesh['aux'=8,'lmo'=4] {'aux','lmo'}, dimensions={0}, use_global_device_ids=true | all-gather | bytes 101376 | tf_op jit(solution)/shard_map/all_gather | solution.py:35
  40.2 0.8 copy.22
  41.0 0.7 iota_compare_fusion.2
  41.7 0.9 fusion.1
  42.7 0.2 copy.23
  42.9 8.5 %convolution_bitcast_fusion = f32[6144,128]{0,1:T(8,128)} fusion(bf16[768,128]{1,0:T(8,128)(2,1)S(1)} %bitcast.30, bf16[6144,768]{1,0:T(8,128)(2,1)} %bitcast.28), kind=kOutput, calls=%fused_computation.1 | convolution fusion | flops 1207959552 | bytes 12779520 | tf_op jit(solution)/shard_map/dot_general | solution.py:39
  51.4 3.6 %copy.24 = f32[6144,128]{1,0:T(8,128)} copy(f32[6144,128]{0,1:T(8,128)} %convolution_bitcast_fusion) | data formatting | bytes 6291456 | tf_op jit(solution)/shard_map/dot_general | solution.py:39
  55.0 0.0 copy-start.2
  55.0 0.0 copy-start.3
  55.0 5.0 %copy.25 = f32[8,6,128,128]{2,1,0,3:T(8,128)} copy(f32[8,6,128,128]{3,2,1,0:T(8,128)} %bitcast.29) | data formatting | bytes 6291456 | tf_op jit(solution)/shard_map/reshape;reshape | solution.py:29
  60.0 0.0 copy-done.2
  60.0 0.1 copy.21
  60.1 0.0 copy-done.3
  60.1 0.1 iota_compare_fusion.3
  60.2 4.5 %fusion = bf16[128,8,3,128]{3,2,1,0:T(4,128)(2,1)S(1)} fusion(f32[8,6,128,128]{2,1,0,3:T(8,128)} %copy.25, s32[128,3]{1,0:T(8,128)S(1)} %copy.21, pred[128,3]{1,0:T(8,128)(4,1)S(1)} %iota_compare_fusion.3), kind=kOutput, calls=%fused_computation.3 | convolution fusion | flops 28709376 | bytes 3934080 | tf_op jit(solution)/shard_map/pbni,ikb->ipkn/dot_general | solution.py:30
  64.7 0.7 convert_element_type.29
  65.4 0.7 gather_fusion
  66.1 0.2 broadcast_select_fusion
  66.4 26.8 %all_to_all.18 = bf16[128,8,384]{2,1,0:T(8,128)(2,1)S(1)} all-to-all(bf16[128,8,384]{2,1,0:T(8,128)(2,1)S(1)} %broadcast_select_fusion), channel_id=1, replica_groups=mesh['aux'=8,'lmo'=4] {'aux','lmo'}, dimensions={0} | all-to-all | bytes 1572864 | tf_op jit(solution)/shard_map/all_to_all | solution.py:46
  93.1 0.0 copy-done
  93.1 0.4 convolution_convert_fusion.1
  93.6 0.0 copy-start.1
  93.6 1.3 %convolution_multiply_fusion = f32[4,256,256]{2,1,0:T(8,128)} fusion(bf16[4,256,256]{2,1,0:T(8,128)(2,1)S(1)} %convolution_convert_fusion.1), kind=kOutput, calls=%fused_computation.4 | convolution fusion | flops 134479872 | bytes 1572864 | tf_op jit(solution)/shard_map/rpa,rpb->rab/dot_general | solution.py:52
  94.9 0.0 copy-done.1
  (2 shorter events, 0.0 us)
Async XLA Ops:
  0.6 92.5 %copy-start = (bf16[4,384,256]{2,1,0:T(8,128)(2,1)S(1)}, bf16[4,384,256]{2,1,0:T(8,128)(2,1)}, u32[]{:S(2)}) copy-start(bf16[4,384,256]{2,1,0:T(8,128)(2,1)} %param.15) | copy-start | bytes 2359300
  55.0 5.0 %copy-start.2 = (s32[128,3]{0,1:T(4,128)S(1)}, s32[128,3]{0,1:T(4,128)}, u32[]{:S(2)}) copy-start(s32[128,3]{0,1:T(4,128)} %param.12) | copy-start | bytes 4612
  55.0 5.1 %copy-start.3 = (s32[128]{0:T(128)S(1)}, s32[128]{0:T(128)}, u32[]{:S(2)}) copy-start(s32[128]{0:T(128)} %param.13) | copy-start | bytes 1540
  93.6 1.3 %copy-start.1 = (bf16[4,256,256]{2,1,0:T(8,128)(2,1)}, bf16[4,256,256]{2,1,0:T(8,128)(2,1)S(1)}, u32[]{:S(2)}) copy-start(bf16[4,256,256]{2,1,0:T(8,128)(2,1)S(1)} %convolution_convert_fusion.1) | copy-start | bytes 1572868
where the time goes:
time: 96.4 us; the launch traced here: 94.9 us
  blocking collectives  64.9 us (67%)
  matrix products  15.7 us (16%)
  local copies, waits for them, and re-layouts  11.2 us (12%)
  other arithmetic  2.43 us (3%)
    all_gather x1, blocking collectives, shards(): all_coef = lax.all_gather(lmo_coef, ('aux', 'lmo'), axis=0, tiled=True)  38.1 us
    all_to_all x1, blocking collectives, shards(): lax.all_to_all(ordered, ('aux', 'lmo'), split_axis=0, concat_axis=1, tile...  26.8 us
    dot_general x1, matrix products, shards(): jnp.dot(aux_ints.reshape(row_total * ao_total, ao_total), dense_coef, pre...  8.53 us
    another operation x1, local copies, waits for them, and re-layouts, select(): tiled = half_ints.reshape(row_total, blocks, BLK, lmo_total)  5.03 us
    dot_general x1, matrix products, select(): jnp.einsum('pbni,ikb->ipkn', tiled, onehot, precision=lax.Precision.HIGHEST)  4.46 us
    dot_general x1, local copies, waits for them, and re-layouts, shards(): jnp.dot(aux_ints.reshape(row_total * ao_total, ao_total), dense_coef, pre...  3.55 us

commit v1 on v0

v1 whole, which is shorter than its diff:
```python
import jax
import jax.numpy as jnp
from jax import lax
from jax.experimental import pallas as pl
from jax.experimental.pallas import tpu as pltpu
from jax.sharding import PartitionSpec as P

BLK = 128
DB = 3
PB = 3
USED = 8
AXES = ("aux", "lmo")


def half_kernel(
    owned, aux_ref, coef_ref, ao_dom_ref, ao_cnt_ref, pao_dom_ref, pao_cnt_ref, order_ref,
    send_ref, flat_ref, tiles_ref,
):
    sources, rows_each, _ = coef_ref.shape
    lmo_total = sources * rows_each
    row_total, ao_total, _ = aux_ref.shape
    blocks = ao_total // BLK
    cols = tiles_ref.shape[0]

    for src in range(sources):
        flat_ref[pl.ds(src * rows_each, rows_each), :] = coef_ref[src].astype(jnp.float32)
    coef_t = flat_ref[...].T

    ao_cnt = ao_cnt_ref[...]
    dense = []
    for b in range(blocks):
        total = jnp.zeros((BLK, lmo_total), jnp.float32)
        for k in range(DB):
            hit = (ao_dom_ref[k : k + 1, :] == b) & (ao_cnt > k)
            total = jnp.where(hit, coef_t[k * BLK : (k + 1) * BLK, :], total)
        dense.append(total)
    dense_t = jnp.concatenate(dense, axis=0).astype(jnp.bfloat16)

    code = pao_cnt_ref[...]
    for k in range(PB):
        code = code + pao_dom_ref[k : k + 1, :] * (4 * 8**k)
    code_col = jnp.broadcast_to(code, (8, lmo_total)).T[:, :1]
    cnt_col = code_col & 3
    lmo_id = lax.broadcasted_iota(jnp.int32, (lmo_total, lmo_total), 0)
    held = order_ref[...] == lmo_id
    cnt_slot = jnp.sum(jnp.where(held, cnt_col, 0), axis=0, keepdims=True)
    slot_id = lax.broadcasted_iota(jnp.int32, (1, lmo_total), 1)
    member = slot_id % owned
    first = (slot_id // owned) * USED
    for step in range(1, owned):
        first = first + jnp.where(member >= step, pltpu.roll(cnt_slot, step, 1), 0)
    first_col = jnp.sum(
        jnp.where(held, first, 0).astype(jnp.float32), axis=1, keepdims=True
    ).astype(jnp.int32)

    col_id = lax.broadcasted_iota(jnp.int32, (lmo_total, cols), 1)
    spread = jnp.zeros((lmo_total, cols), jnp.bool_)
    wanted = jnp.zeros((lmo_total, cols), jnp.int32)
    for k in range(PB):
        here = (col_id == first_col + k) & (cnt_col > k)
        wanted = jnp.where(here, (code_col >> (2 + 3 * k)) & 7, wanted)
        spread = spread | here
    block_row = jnp.sum(wanted, axis=0, keepdims=True)
    spread = jnp.where(spread, 1.0, 0.0).astype(jnp.bfloat16)
    weights = jnp.dot(dense_t, spread, preferred_element_type=jnp.float32).astype(jnp.bfloat16)

    for p in range(row_total):
        half = jnp.dot(aux_ref[p], weights, preferred_element_type=jnp.float32)
        picked = half[:BLK]
        for b in range(1, blocks):
            picked = jnp.where(block_row == b, half[b * BLK : (b + 1) * BLK], picked)
        tiles_ref[:, p, :] = picked.T
    for col in range(cols):
        dev, slot = divmod(col, USED)
        send_ref[dev, :, slot * BLK : (slot + 1) * BLK] = tiles_ref[col].astype(jnp.bfloat16)


def pair_kernel(owned, aux_total, me_ref, order_ref, cnt_ref, rows_ref, coef_ref, pair_ref, metric_ref):
    slot = 0
    for r in range(owned):
        count = cnt_ref[order_ref[me_ref[0] * owned + r]]
        parts = []
        for k in range(PB):
            at = pl.multiple_of(jnp.minimum(slot + k, USED - 1) * BLK, BLK)
            part = rows_ref[:, pl.ds(at, BLK)]
            parts.append(jnp.where(count > k, part, jnp.zeros_like(part)))
        slot = slot + count
        rows = jnp.concatenate(parts, axis=1)
        pair = jnp.dot(rows, coef_ref[r], preferred_element_type=jnp.float32).astype(jnp.bfloat16)
        pair_ref[r] = pair
        metric = lax.dot_general(
            pair, pair, (((0,), (0,)), ((), ())), preferred_element_type=jnp.float32
        )
        metric_ref[r] = metric / aux_total


def shards(aux_ints, lmo_coef, ao_domain, ao_count, pao_domain, pao_count, owner_order, pao_coef):
    devices = lax.axis_size(AXES)
    rows_each = lmo_coef.shape[0]
    lmo_total = devices * rows_each
    row_total, ao_total, _ = aux_ints.shape
    owned = pao_coef.shape[0]
    aux_total = devices * row_total
    cols = devices * USED

    coef = lax.all_to_all(
        jnp.broadcast_to(lmo_coef[None], (devices,) + lmo_coef.shape), AXES, split_axis=0, concat_axis=0, tiled=True
    )
    vmem = pl.BlockSpec(memory_space=pltpu.VMEM)
    smem = pl.BlockSpec(memory_space=pltpu.SMEM)
    send = pl.pallas_call(
        lambda *refs: half_kernel(owned, *refs),
        out_shape=jax.ShapeDtypeStruct((devices, row_total, USED * BLK), jnp.bfloat16),
        in_specs=[vmem] * 7,
        out_specs=vmem,
        scratch_shapes=[
            pltpu.VMEM((lmo_total, DB * BLK), jnp.float32),
            pltpu.VMEM((cols, row_total, BLK), jnp.float32),
        ],
        compiler_params=pltpu.CompilerParams(vmem_limit_bytes=60 * 2**20),
        cost_estimate=pl.CostEstimate(
            flops=2 * row_total * ao_total * ao_total * cols, bytes_accessed=2 * aux_ints.size, transcendentals=0
        ),
        name="half_transform",
    )(
        aux_ints, coef, ao_domain.T, ao_count[None], pao_domain.T, pao_count[None], owner_order[None]
    )
    received = lax.all_to_all(send, AXES, split_axis=0, concat_axis=0, tiled=True)
    return pl.pallas_call(
        lambda *refs: pair_kernel(owned, aux_total, *refs),
        out_shape=(
            jax.ShapeDtypeStruct((owned, aux_total, pao_coef.shape[2]), jnp.bfloat16),
            jax.ShapeDtypeStruct((owned, pao_coef.shape[2], pao_coef.shape[2]), jnp.float32),
        ),
        in_specs=[smem] * 3 + [vmem] * 2,
        out_specs=(vmem, vmem),
        name="pair_transform",
    )(
        lax.axis_index(AXES)[None].astype(jnp.int32), owner_order, pao_count,
        received.reshape(aux_total, USED * BLK), pao_coef,
    )


def solution(mesh):
    placed = (
        P(AXES, None, None),
        P(AXES, None),
        P(),
        P(),
        P(),
        P(),
        P(),
        P(AXES, None, None),
    )
    return jax.shard_map(
        shards,
        mesh=mesh,
        in_specs=placed,
        out_specs=(P(AXES, None, None), P(AXES, None, None)),
        check_vma=False,
    )
```

time: 96.4 us -> 47.8 us (0.50)
  the two profiles are of different devices: /device:TPU:5 before, /device:TPU:0 now
where the time goes in v1:
time: 47.8 us; the launch traced here: 47.5 us
  waiting for transfers between devices  15.6 us (33%)
  blocking collectives  15 us (31%)
  Pallas kernels  12.1 us (25%)
  starting transfers between devices  2.61 us (5%)
  local copies, waits for them, and re-layouts  1.51 us (3%)
  between operations  0.65 us (1%)
    all_to_all x1, waiting for transfers between devices, shards(): lax.all_to_all(send, AXES, split_axis=0, concat_axis=0, tiled=True)  15.6 us
    all_to_all x1, blocking collectives, shards(): lax.all_to_all(jnp.broadcast_to(lmo_coef[None], (devices,) + lmo_coef.sha...  15 us
    pallas_call x1, Pallas kernels, shards(): pl.pallas_call(lambda *refs: half_kernel(owned, *refs), out_shape=jax.Sha...  8.22 us
    pallas_call x1, Pallas kernels, shards(): pl.pallas_call(lambda *refs: pair_kernel(owned, aux_total, *refs), out_sh...  3.85 us
    all_to_all x1, starting transfers between devices, shards(): lax.all_to_all(send, AXES, split_axis=0, concat_axis=0, tiled=True)  2.61 us
  transfers between devices with their start and end apart: 1, of which 1 were waited for; matrix products, arithmetic and copies ran while one was open for 0% of the time, Pallas kernels for 0%

profile of v1, /device:TPU:0, one launch (start us, length us, event | category | flops | bytes accessed | tf_op | source)
XLA Modules:
  0.0 47.5 jit_solution(11998527566071593979)
XLA Ops:
  0.6 0.7 %broadcast_in_dim.19 = bf16[32,4,384]{2,1,0:T(4,128)(2,1)S(1)} broadcast(bf16[4,384]{1,0:T(4,128)(2,1)} %param.9), dimensions={1,2} | broadcast | bytes 101376 | tf_op jit(solution)/shard_map/broadcast_in_dim | solution.py:107
  1.3 15.0 %all_to_all.10.refs_1_ = bf16[32,4,384]{2,1,0:T(4,128)(2,1)} all-to-all(bf16[32,4,384]{2,1,0:T(4,128)(2,1)S(1)} %broadcast_in_dim.19), channel_id=1, replica_groups=mesh['aux'=8,'lmo'=4] {'aux','lmo'}, dimensions={0} | all-to-all | bytes 196608 | tf_op jit(solution)/shard_map/all_to_all | solution.py:106
  16.4 8.2 %half_transform.1 = bf16[32,8,1024]{2,1,0:T(8,128)(2,1)} custom-call(bf16[8,768,768]{2,1,0:T(8,128)(2,1)} %refs_0_.1, bf16[32,4,384]{2,1,0:T(4,128)(2,1)} %all_to_all.10.refs_1_, s32[3,128]{1,0:T(4,128)} %bitcast.8, s32[1,128]{1,0:T(1,128)} %bitcast.12, s32[3,128]{1,0:T(4,128)} %bitcast.9, s32[1,128]{1,0:T(1,128)} %bitcast.11, s32[1,128]{1,0:T(1,128)} %bitcast.10), custom_call_target="tpu_custom_call" | custom-call | flops 2415919104 | bytes 9437184 | tf_op jit(solution)/shard_map/half_transform/pallas_call | solution.py:111
  24.6 2.6 %all-to-all-start.1 = ((bf16[32,8,1024]{2,1,0:T(8,128)(2,1)}), bf16[32,8,1024]{2,1,0:T(8,128)(2,1)S(1)}, u32[]{:S(2)}, u32[]{:S(2)}) async-start(bf16[32,8,1024]{2,1,0:T(8,128)(2,1)} %half_transform.1), calls=%async_computation.1 | async-start | bytes 1048576 | tf_op jit(solution)/shard_map/all_to_all | solution.py:128
  27.2 15.6 %all-to-all-done.1 = bf16[32,8,1024]{2,1,0:T(8,128)(2,1)S(1)} async-done(((bf16[32,8,1024]{2,1,0:T(8,128)(2,1)}), bf16[32,8,1024]{2,1,0:T(8,128)(2,1)S(1)}, u32[]{:S(2)}, u32[]{:S(2)}) %all-to-all-start.1) | async-done | bytes 524320 | tf_op jit(solution)/shard_map/all_to_all | solution.py:128
  42.8 0.0 copy-start
  42.8 0.8 %copy-done = bf16[32,8,1024]{2,1,0:T(8,128)(2,1)} copy-done((bf16[32,8,1024]{2,1,0:T(8,128)(2,1)}, bf16[32,8,1024]{2,1,0:T(8,128)(2,1)S(1)}, u32[]{:S(2)}) %copy-start) | copy-done | bytes 524312
  43.6 3.9 %pair_transform.1 = (bf16[4,256,256]{2,1,0:T(8,128)(2,1)}, f32[4,256,256]{2,1,0:T(8,128)}) custom-call(s32[1]{0:T(128)} %bitcast.refs_0_, s32[128]{0:T(128)} %refs_1_.1, s32[128]{0:T(128)} %refs_2_.1, bf16[256,1024]{1,0:T(8,128)(2,1)} %bitcast.7, bf16[4,384,256]{2,1,0:T(8,128)(2,1)} %refs_4_.1), custom_call_target="tpu_custom_call" | custom-call | tf_op jit(solution)/shard_map/pair_transform/pallas_call | solution.py:129
Async XLA Ops:
  24.6 18.2 %all-to-all-start.1 = ((bf16[32,8,1024]{2,1,0:T(8,128)(2,1)}), bf16[32,8,1024]{2,1,0:T(8,128)(2,1)S(1)}, u32[]{:S(2)}, u32[]{:S(2)}) async-start(bf16[32,8,1024]{2,1,0:T(8,128)(2,1)} %half_transform.1), calls=%async_computation.1 | async-start | bytes 1048576 | tf_op jit(solution)/shard_map/all_to_all | solution.py:128
  42.8 0.8 %copy-start = (bf16[32,8,1024]{2,1,0:T(8,128)(2,1)}, bf16[32,8,1024]{2,1,0:T(8,128)(2,1)S(1)}, u32[]{:S(2)}) copy-start(bf16[32,8,1024]{2,1,0:T(8,128)(2,1)S(1)} %all-to-all-done.1) | copy-start | bytes 1572868

commit v2 on v1

--- a/solution.py
+++ b/solution.py
@@ -12,29 +12,27 @@
 AXES = ("aux", "lmo")
 
 
-def half_kernel(
-    owned, aux_ref, coef_ref, ao_dom_ref, ao_cnt_ref, pao_dom_ref, pao_cnt_ref, order_ref,
-    send_ref, flat_ref, tiles_ref,
+def prep_kernel(
+    owned, used, coef_hbm, ao_dom_hbm, ao_cnt_hbm, pao_dom_hbm, pao_cnt_hbm, order_hbm,
+    bcast_ref, spread_ref, table_ref,
+    coef_ref, ao_dom_ref, ao_cnt_ref, pao_dom_ref, pao_cnt_ref, order_ref, sems,
 ):
-    sources, rows_each, _ = coef_ref.shape
-    lmo_total = sources * rows_each
-    row_total, ao_total, _ = aux_ref.shape
-    blocks = ao_total // BLK
-    cols = tiles_ref.shape[0]
-
-    for src in range(sources):
-        flat_ref[pl.ds(src * rows_each, rows_each), :] = coef_ref[src].astype(jnp.float32)
-    coef_t = flat_ref[...].T
-
-    ao_cnt = ao_cnt_ref[...]
-    dense = []
-    for b in range(blocks):
-        total = jnp.zeros((BLK, lmo_total), jnp.float32)
-        for k in range(DB):
-            hit = (ao_dom_ref[k : k + 1, :] == b) & (ao_cnt > k)
-            total = jnp.where(hit, coef_t[k * BLK : (k + 1) * BLK, :], total)
-        dense.append(total)
-    dense_t = jnp.concatenate(dense, axis=0).astype(jnp.bfloat16)
+    copies = [
+        pltpu.make_async_copy(src, dst, sems.at[n])
+        for n, (src, dst) in enumerate((
+            (coef_hbm, coef_ref), (ao_dom_hbm, ao_dom_ref), (ao_cnt_hbm, ao_cnt_ref),
+            (pao_dom_hbm, pao_dom_ref), (pao_cnt_hbm, pao_cnt_ref), (order_hbm, order_ref),
+        ))
+    ]
+    for copy in copies:
+        copy.start()
+    for copy in copies:
+        copy.wait()
+    devices = bcast_ref.shape[0]
+    lmo_total, cols = spread_ref.shape
+    own = coef_ref[...]
+    for dev in range(devices):
+        bcast_ref[dev] = own
 
     code = pao_cnt_ref[...]
     for k in range(PB):
@@ -46,7 +44,7 @@
     cnt_slot = jnp.sum(jnp.where(held, cnt_col, 0), axis=0, keepdims=True)
     slot_id = lax.broadcasted_iota(jnp.int32, (1, lmo_total), 1)
     member = slot_id % owned
-    first = (slot_id // owned) * USED
+    first = (slot_id // owned) * used
     for step in range(1, owned):
         first = first + jnp.where(member >= step, pltpu.roll(cnt_slot, step, 1), 0)
     first_col = jnp.sum(
@@ -60,10 +58,36 @@
         here = (col_id == first_col + k) & (cnt_col > k)
         wanted = jnp.where(here, (code_col >> (2 + 3 * k)) & 7, wanted)
         spread = spread | here
-    block_row = jnp.sum(wanted, axis=0, keepdims=True)
-    spread = jnp.where(spread, 1.0, 0.0).astype(jnp.bfloat16)
-    weights = jnp.dot(dense_t, spread, preferred_element_type=jnp.float32).astype(jnp.bfloat16)
-
+    spread_ref[...] = jnp.where(spread, 1.0, 0.0).astype(jnp.bfloat16)
+    table_ref[0:1, :] = jnp.sum(wanted, axis=0, keepdims=True)
+    for k in range(DB):
+        block = jnp.where(ao_cnt_ref[...] > k, ao_dom_ref[k : k + 1, :], -1)
+        table_ref[1 + k : 2 + k, :lmo_total] = block
+
+
+def half_kernel(aux_ref, coef_ref, spread_ref, table_ref, send_ref, flat_ref, tiles_ref):
+    sources, rows_each, _ = coef_ref.shape
+    lmo_total, cols = spread_ref.shape
+    devices, row_total, width = send_ref.shape
+    used = width // BLK
+    blocks = aux_ref.shape[1] // BLK
+
+    for src in range(sources):
+        flat_ref[pl.ds(src * rows_each, rows_each), :] = coef_ref[src].astype(jnp.float32)
+    coef_t = flat_ref[...].T
+    dense = []
+    for b in range(blocks):
+        total = jnp.zeros((BLK, lmo_total), jnp.float32)
+        for k in range(DB):
+            hit = table_ref[1 + k : 2 + k, :lmo_total] == b
+            total = jnp.where(hit, coef_t[k * BLK : (k + 1) * BLK, :], total)
+        dense.append(total)
+    dense_t = jnp.concatenate(dense, axis=0).astype(jnp.bfloat16)
+    weights = jnp.dot(
+        dense_t, spread_ref[...], preferred_element_type=jnp.float32
+    ).astype(jnp.bfloat16)
+
+    block_row = table_ref[0:1, :]
     for p in range(row_total):
         half = jnp.dot(aux_ref[p], weights, preferred_element_type=jnp.float32)
         picked = half[:BLK]
@@ -71,7 +95,7 @@
             picked = jnp.where(block_row == b, half[b * BLK : (b + 1) * BLK], picked)
         tiles_ref[:, p, :] = picked.T
     for col in range(cols):
-        dev, slot = divmod(col, USED)
+        dev, slot = divmod(col, used)
         send_ref[dev, :, slot * BLK : (slot + 1) * BLK] = tiles_ref[col].astype(jnp.bfloat16)
 
 
@@ -103,28 +127,50 @@
     aux_total = devices * row_total
     cols = devices * USED
 
-    coef = lax.all_to_all(
-        jnp.broadcast_to(lmo_coef[None], (devices,) + lmo_coef.shape), AXES, split_axis=0, concat_axis=0, tiled=True
-    )
     vmem = pl.BlockSpec(memory_space=pltpu.VMEM)
     smem = pl.BlockSpec(memory_space=pltpu.SMEM)
+    small = pltpu.CompilerParams(vmem_limit_bytes=16 * 2**20)
+    bcast, spread, table = pl.pallas_call(
+        lambda *refs: prep_kernel(owned, USED, *refs),
+        out_shape=(
+            jax.ShapeDtypeStruct((devices,) + lmo_coef.shape, jnp.bfloat16),
+            jax.ShapeDtypeStruct((lmo_total, cols), jnp.bfloat16),
+            jax.ShapeDtypeStruct((8, cols), jnp.int32),
+        ),
+        in_specs=[pl.BlockSpec(memory_space=pltpu.HBM)] * 6,
+        out_specs=(vmem,) * 3,
+        scratch_shapes=[
+            pltpu.VMEM(lmo_coef.shape, jnp.bfloat16),
+            pltpu.VMEM((DB, lmo_total), jnp.int32),
+            pltpu.VMEM((1, lmo_total), jnp.int32),
+            pltpu.VMEM((PB, lmo_total), jnp.int32),
+            pltpu.VMEM((1, lmo_total), jnp.int32),
+            pltpu.VMEM((1, lmo_total), jnp.int32),
+            pltpu.SemaphoreType.DMA((6,)),
+        ],
+        compiler_params=small,
+        cost_estimate=pl.CostEstimate(flops=2 * 10**10, bytes_accessed=2**18, transcendentals=0),
+        name="prep",
+    )(*(
+        pltpu.with_memory_space_constraint(x, pltpu.HBM)
+        for x in (lmo_coef, ao_domain.T, ao_count[None], pao_domain.T, pao_count[None], owner_order[None])
+    ))
+    coef = lax.all_to_all(bcast, AXES, split_axis=0, concat_axis=0, tiled=True)
     send = pl.pallas_call(
-        lambda *refs: half_kernel(owned, *refs),
+        half_kernel,
         out_shape=jax.ShapeDtypeStruct((devices, row_total, USED * BLK), jnp.bfloat16),
-        in_specs=[vmem] * 7,
+        in_specs=[vmem] * 4,
         out_specs=vmem,
         scratch_shapes=[
             pltpu.VMEM((lmo_total, DB * BLK), jnp.float32),
             pltpu.VMEM((cols, row_total, BLK), jnp.float32),
         ],
-        compiler_params=pltpu.CompilerParams(vmem_limit_bytes=60 * 2**20),
+        compiler_params=pltpu.CompilerParams(vmem_limit_bytes=24 * 2**20),
         cost_estimate=pl.CostEstimate(
             flops=2 * row_total * ao_total * ao_total * cols, bytes_accessed=2 * aux_ints.size, transcendentals=0
         ),
         name="half_transform",
-    )(
-        aux_ints, coef, ao_domain.T, ao_count[None], pao_domain.T, pao_count[None], owner_order[None]
-    )
+    )(aux_ints, coef, spread, table)
     received = lax.all_to_all(send, AXES, split_axis=0, concat_axis=0, tiled=True)
     return pl.pallas_call(
         lambda *refs: pair_kernel(owned, aux_total, *refs),
@@ -134,6 +180,7 @@
         ),
         in_specs=[smem] * 3 + [vmem] * 2,
         out_specs=(vmem, vmem),
+        compiler_params=small,
         name="pair_transform",
     )(
         lax.axis_index(AXES)[None].astype(jnp.int32), owner_order, pao_count,

time: 47.8 us -> 42.8 us (0.90)
  Pallas kernels: 12.1 us -> 8.7 us
  local copies, waits for them, and re-layouts: 1.51 us -> 0.02 us
    pallas_call x1 -> x2, Pallas kernels: 8.22 us -> 5.61 us  [the longest x1 4.21 us: shards(): pl.pallas_call(half_kernel, out_shape=jax.ShapeDtypeStruct((devices, row_...]
    unnamed x2 -> x8, local copies, waits for them, and re-layouts: 0.79 us -> 0.02 us
    pallas_call x1, Pallas kernels: 3.85 us -> 3.09 us  [shards(): pl.pallas_call(lambda *refs: pair_kernel(owned, aux_total, *refs), out_sh...]
    broadcast_in_dim x1 -> x0, local copies, waits for them, and re-layouts: 0.71 us -> none  [shards(): jnp.broadcast_to(lmo_coef[None], (devices,) + lmo_coef.shape)]
where the time goes in v2:
time: 42.8 us; the launch traced here: 42.5 us
  waiting for transfers between devices  15.6 us (36%)
  blocking collectives  14.9 us (35%)
  Pallas kernels  8.7 us (20%)
  starting transfers between devices  2.61 us (6%)
  between operations  0.69 us (2%)
    all_to_all x1, waiting for transfers between devices, shards(): lax.all_to_all(send, AXES, split_axis=0, concat_axis=0, tiled=True)  15.6 us
    all_to_all x1, blocking collectives, shards(): coef = lax.all_to_all(bcast, AXES, split_axis=0, concat_axis=0, tiled=True)  14.9 us
    pallas_call x1, Pallas kernels, shards(): pl.pallas_call(half_kernel, out_shape=jax.ShapeDtypeStruct((devices, row_...  4.21 us
    pallas_call x1, Pallas kernels, shards(): pl.pallas_call(lambda *refs: pair_kernel(owned, aux_total, *refs), out_sh...  3.09 us
    all_to_all x1, starting transfers between devices, shards(): lax.all_to_all(send, AXES, split_axis=0, concat_axis=0, tiled=True)  2.61 us
    pallas_call x1, Pallas kernels, shards(): pl.pallas_call(lambda *refs: prep_kernel(owned, USED, *refs), out_shape=(...  1.4 us
  transfers between devices with their start and end apart: 1, of which 1 were waited for; matrix products, arithmetic and copies ran while one was open for 0% of the time, Pallas kernels for 0%

profile of v2, /device:TPU:0, one launch (start us, length us, event | category | flops | bytes accessed | tf_op | source)
XLA Modules:
  0.0 42.5 jit_solution(11258295179216638498)
XLA Ops:
  0.6 0.0 copy-start
  0.6 1.4 %prep.1 = (bf16[32,4,384]{2,1,0:T(4,128)(2,1)S(1)}, bf16[128,256]{1,0:T(8,128)(2,1)S(1)}, s32[8,256]{1,0:T(8,128)S(1)}) custom-call(bf16[4,384]{1,0:T(4,128)(2,1)} %refs_0_.1, s32[3,128]{1,0:T(4,128)} %bitcast.10, s32[1,128]{1,0:T(1,128)} %bitcast.12, s32[3,128]{1,0:T(4,128)} %bitcast.11, s32[1,128]{1,0:T(1,128)} %bitcast.9, s32[1,128]{1,0:T(1,128)} %bitcast.8), custom_call_target="tpu_custom_call" | custom-call | flops 20000000000 | bytes 262144 | tf_op jit(solution)/shard_map/prep/pallas_call | solution.py:133
  2.0 0.0 copy-start.1
  2.1 0.0 copy-start.2
  2.1 0.0 copy-start.3
  2.1 14.9 %all_to_all.10.coef_ref = bf16[32,4,384]{2,1,0:T(4,128)(2,1)S(1)} all-to-all(bf16[32,4,384]{2,1,0:T(4,128)(2,1)S(1)} %get-tuple-element.5), channel_id=1, replica_groups=mesh['aux'=8,'lmo'=4] {'aux','lmo'}, dimensions={0} | all-to-all | bytes 196608 | tf_op jit(solution)/shard_map/all_to_all | solution.py:158
  17.0 0.0 copy-done
  17.0 4.2 %half_transform.1 = bf16[32,8,1024]{2,1,0:T(8,128)(2,1)} custom-call(bf16[8,768,768]{2,1,0:T(8,128)(2,1)S(1)} %copy-done, bf16[32,4,384]{2,1,0:T(4,128)(2,1)S(1)} %all_to_all.10.coef_ref, bf16[128,256]{1,0:T(8,128)(2,1)S(1)} %get-tuple-element.6.spread_ref, s32[8,256]{1,0:T(8,128)S(1)} %get-tuple-element.7.table_ref), custom_call_target="tpu_custom_call" | custom-call | flops 2415919104 | bytes 9437184 | tf_op jit(solution)/shard_map/half_transform/pallas_call | solution.py:159
  21.2 2.6 %all-to-all-start.1 = ((bf16[32,8,1024]{2,1,0:T(8,128)(2,1)}), bf16[32,8,1024]{2,1,0:T(8,128)(2,1)S(1)}, u32[]{:S(2)}, u32[]{:S(2)}) async-start(bf16[32,8,1024]{2,1,0:T(8,128)(2,1)} %half_transform.1), calls=%async_computation.1 | async-start | bytes 1048576 | tf_op jit(solution)/shard_map/all_to_all | solution.py:174
  23.8 15.6 %all-to-all-done.1 = bf16[32,8,1024]{2,1,0:T(8,128)(2,1)S(1)} async-done(((bf16[32,8,1024]{2,1,0:T(8,128)(2,1)}), bf16[32,8,1024]{2,1,0:T(8,128)(2,1)S(1)}, u32[]{:S(2)}, u32[]{:S(2)}) %all-to-all-start.1) | async-done | bytes 524320 | tf_op jit(solution)/shard_map/all_to_all | solution.py:174
  39.4 0.0 copy-done.1
  39.4 0.0 copy-done.2
  39.5 0.0 copy-done.3
  39.5 3.1 %pair_transform.1 = (bf16[4,256,256]{2,1,0:T(8,128)(2,1)}, f32[4,256,256]{2,1,0:T(8,128)}) custom-call(s32[1]{0:T(128)} %bitcast.refs_0_, s32[128]{0:T(128)S(1)} %copy-done.2, s32[128]{0:T(128)S(1)} %copy-done.3, bf16[256,1024]{1,0:T(8,128)(2,1)S(1)} %bitcast.7, bf16[4,384,256]{2,1,0:T(8,128)(2,1)S(1)} %copy-done.1), custom_call_target="tpu_custom_call" | custom-call | tf_op jit(solution)/shard_map/pair_transform/pallas_call | solution.py:175
Async XLA Ops:
  0.6 16.4 %copy-start = (bf16[8,768,768]{2,1,0:T(8,128)(2,1)S(1)}, bf16[8,768,768]{2,1,0:T(8,128)(2,1)}, u32[]{:S(2)}) copy-start(bf16[8,768,768]{2,1,0:T(8,128)(2,1)} %aux_ref.1) | copy-start | bytes 28311556
  2.0 37.4 %copy-start.1 = (bf16[4,384,256]{2,1,0:T(8,128)(2,1)S(1)}, bf16[4,384,256]{2,1,0:T(8,128)(2,1)}, u32[]{:S(2)}) copy-start(bf16[4,384,256]{2,1,0:T(8,128)(2,1)} %refs_4_.1) | copy-start | bytes 2359300
  2.1 37.4 %copy-start.2 = (s32[128]{0:T(128)S(1)}, s32[128]{0:T(128)}, u32[]{:S(2)}) copy-start(s32[128]{0:T(128)} %refs_1_.1) | copy-start | bytes 1540
  2.1 37.4 %copy-start.3 = (s32[128]{0:T(128)S(1)}, s32[128]{0:T(128)}, u32[]{:S(2)}) copy-start(s32[128]{0:T(128)} %refs_2_.1) | copy-start | bytes 1540
  21.2 18.2 %all-to-all-start.1 = ((bf16[32,8,1024]{2,1,0:T(8,128)(2,1)}), bf16[32,8,1024]{2,1,0:T(8,128)(2,1)S(1)}, u32[]{:S(2)}, u32[]{:S(2)}) async-start(bf16[32,8,1024]{2,1,0:T(8,128)(2,1)} %half_transform.1), calls=%async_computation.1 | async-start | bytes 1048576 | tf_op jit(solution)/shard_map/all_to_all | solution.py:174

commit v3 on v2

--- a/solution.py
+++ b/solution.py
@@ -14,7 +14,7 @@
 
 def prep_kernel(
     owned, used, coef_hbm, ao_dom_hbm, ao_cnt_hbm, pao_dom_hbm, pao_cnt_hbm, order_hbm,
-    bcast_ref, spread_ref, table_ref,
+    bcast_ref, spread_ref, table_ref, counts_ref,
     coef_ref, ao_dom_ref, ao_cnt_ref, pao_dom_ref, pao_cnt_ref, order_ref, sems,
 ):
     copies = [
@@ -63,6 +63,11 @@
     for k in range(DB):
         block = jnp.where(ao_cnt_ref[...] > k, ao_dom_ref[k : k + 1, :], -1)
         table_ref[1 + k : 2 + k, :lmo_total] = block
+    mine = lax.axis_index(AXES) * owned
+    for r in range(owned):
+        here = jnp.where(slot_id == mine + r, cnt_slot, 0)
+        count = jnp.sum(here.astype(jnp.float32), axis=1, keepdims=True)
+        counts_ref[r : r + 1, :] = jnp.broadcast_to(count, (1, 128)).astype(jnp.int32)
 
 
 def half_kernel(aux_ref, coef_ref, spread_ref, table_ref, send_ref, flat_ref, tiles_ref):
@@ -99,23 +104,32 @@
         send_ref[dev, :, slot * BLK : (slot + 1) * BLK] = tiles_ref[col].astype(jnp.bfloat16)
 
 
-def pair_kernel(owned, aux_total, me_ref, order_ref, cnt_ref, rows_ref, coef_ref, pair_ref, metric_ref):
+def pair_kernel(counts_ref, rows_ref, coef_ref, pair_hbm, metric_hbm, pair_ref, metric_ref, sems):
+    owned, aux_total, _ = pair_ref.shape
+    used = rows_ref.shape[1] // BLK
+    counts = [counts_ref[r : r + 1, :][0, 0] for r in range(owned)]
+    copies = []
     slot = 0
     for r in range(owned):
-        count = cnt_ref[order_ref[me_ref[0] * owned + r]]
         parts = []
         for k in range(PB):
-            at = pl.multiple_of(jnp.minimum(slot + k, USED - 1) * BLK, BLK)
+            at = pl.multiple_of(jnp.minimum(slot + k, used - 1) * BLK, BLK)
             part = rows_ref[:, pl.ds(at, BLK)]
-            parts.append(jnp.where(count > k, part, jnp.zeros_like(part)))
-        slot = slot + count
+            parts.append(jnp.where(counts[r] > k, part, jnp.zeros_like(part)))
+        slot = slot + counts[r]
         rows = jnp.concatenate(parts, axis=1)
         pair = jnp.dot(rows, coef_ref[r], preferred_element_type=jnp.float32).astype(jnp.bfloat16)
         pair_ref[r] = pair
+        copies.append(pltpu.make_async_copy(pair_ref.at[r], pair_hbm.at[r], sems.at[0, r]))
+        copies[-1].start()
         metric = lax.dot_general(
             pair, pair, (((0,), (0,)), ((), ())), preferred_element_type=jnp.float32
         )
         metric_ref[r] = metric / aux_total
+        copies.append(pltpu.make_async_copy(metric_ref.at[r], metric_hbm.at[r], sems.at[1, r]))
+        copies[-1].start()
+    for copy in copies:
+        copy.wait()
 
 
 def shards(aux_ints, lmo_coef, ao_domain, ao_count, pao_domain, pao_count, owner_order, pao_coef):
@@ -128,17 +142,17 @@
     cols = devices * USED
 
     vmem = pl.BlockSpec(memory_space=pltpu.VMEM)
-    smem = pl.BlockSpec(memory_space=pltpu.SMEM)
     small = pltpu.CompilerParams(vmem_limit_bytes=16 * 2**20)
-    bcast, spread, table = pl.pallas_call(
+    bcast, spread, table, counts = pl.pallas_call(
         lambda *refs: prep_kernel(owned, USED, *refs),
         out_shape=(
             jax.ShapeDtypeStruct((devices,) + lmo_coef.shape, jnp.bfloat16),
             jax.ShapeDtypeStruct((lmo_total, cols), jnp.bfloat16),
             jax.ShapeDtypeStruct((8, cols), jnp.int32),
+            jax.ShapeDtypeStruct((owned, 128), jnp.int32),
         ),
         in_specs=[pl.BlockSpec(memory_space=pltpu.HBM)] * 6,
-        out_specs=(vmem,) * 3,
+        out_specs=(vmem,) * 4,
         scratch_shapes=[
             pltpu.VMEM(lmo_coef.shape, jnp.bfloat16),
             pltpu.VMEM((DB, lmo_total), jnp.int32),
@@ -172,20 +186,19 @@
         name="half_transform",
     )(aux_ints, coef, spread, table)
     received = lax.all_to_all(send, AXES, split_axis=0, concat_axis=0, tiled=True)
+    outs = (
+        ((owned, aux_total, pao_coef.shape[2]), jnp.bfloat16),
+        ((owned, pao_coef.shape[2], pao_coef.shape[2]), jnp.float32),
+    )
     return pl.pallas_call(
-        lambda *refs: pair_kernel(owned, aux_total, *refs),
-        out_shape=(
-            jax.ShapeDtypeStruct((owned, aux_total, pao_coef.shape[2]), jnp.bfloat16),
-            jax.ShapeDtypeStruct((owned, pao_coef.shape[2], pao_coef.shape[2]), jnp.float32),
-        ),
-        in_specs=[smem] * 3 + [vmem] * 2,
-        out_specs=(vmem, vmem),
+        pair_kernel,
+        out_shape=tuple(jax.ShapeDtypeStruct(*out) for out in outs),
+        in_specs=[vmem] * 3,
+        out_specs=(pl.BlockSpec(memory_space=pltpu.HBM),) * 2,
+        scratch_shapes=[pltpu.VMEM(*out) for out in outs] + [pltpu.SemaphoreType.DMA((2, owned))],
         compiler_params=small,
         name="pair_transform",
-    )(
-        lax.axis_index(AXES)[None].astype(jnp.int32), owner_order, pao_count,
-        received.reshape(aux_total, USED * BLK), pao_coef,
-    )
+    )(counts, received.reshape(aux_total, USED * BLK), pao_coef)
 
 
 def solution(mesh):

time: 42.8 us -> 40.3 us (0.942)
  blocking collectives: 14.9 us -> 32.3 us
  waiting for transfers between devices: 15.6 us -> 0 us
  starting transfers between devices: 2.61 us -> 0 us
  Pallas kernels: 8.7 us -> 7.18 us
    all_to_all x0 -> x1, blocking collectives: none -> 17.3 us  [shards(): lax.all_to_all(send, AXES, split_axis=0, concat_axis=0, tiled=True)]
    all_to_all x1 -> x0, waiting for transfers between devices: 15.6 us -> none  [shards(): lax.all_to_all(send, AXES, split_axis=0, concat_axis=0, tiled=True)]
    all_to_all x1 -> x0, starting transfers between devices: 2.61 us -> none  [shards(): lax.all_to_all(send, AXES, split_axis=0, concat_axis=0, tiled=True)]
    pallas_call x1, Pallas kernels: 4.21 us -> 3.4 us  [shards(): pl.pallas_call(half_kernel, out_shape=jax.ShapeDtypeStruct((devices, row_...]
    pallas_call x1, Pallas kernels: 3.09 us -> 2.38 us  [shards(): pl.pallas_call(pair_kernel, out_shape=tuple((jax.ShapeDtypeStruct(*out) f...]
  transfers between devices with their start and end apart: 1 -> 0, of which waited for: 1 -> 0; matrix products, arithmetic and copies ran while one was open for 0% -> 0% of each run, Pallas kernels for 0% -> 0%
where the time goes in v3:
time: 40.3 us; the launch traced here: 40.1 us
  blocking collectives  32.3 us (80%)
  Pallas kernels  7.18 us (18%)
  between operations  0.66 us (2%)
    all_to_all x1, blocking collectives, shards(): lax.all_to_all(send, AXES, split_axis=0, concat_axis=0, tiled=True)  17.3 us
    all_to_all x1, blocking collectives, shards(): coef = lax.all_to_all(bcast, AXES, split_axis=0, concat_axis=0, tiled=True)  14.9 us
    pallas_call x1, Pallas kernels, shards(): pl.pallas_call(half_kernel, out_shape=jax.ShapeDtypeStruct((devices, row_...  3.4 us
    pallas_call x1, Pallas kernels, shards(): pl.pallas_call(pair_kernel, out_shape=tuple((jax.ShapeDtypeStruct(*out) f...  2.38 us
    pallas_call x1, Pallas kernels, shards(): pl.pallas_call(lambda *refs: prep_kernel(owned, USED, *refs), out_shape=(...  1.4 us

profile of v3, /device:TPU:0, one launch (start us, length us, event | category | flops | bytes accessed | tf_op | source)
XLA Modules:
  0.0 40.1 jit_solution(7750724900837580831)
XLA Ops:
  0.6 0.0 copy-start
  0.6 1.4 %prep.1 = (bf16[32,4,384]{2,1,0:T(4,128)(2,1)S(1)}, bf16[128,256]{1,0:T(8,128)(2,1)S(1)}, s32[8,256]{1,0:T(8,128)S(1)}, s32[4,128]{1,0:T(4,128)S(1)}) custom-call(bf16[4,384]{1,0:T(4,128)(2,1)} %refs_0_.1, s32[3,128]{1,0:T(4,128)} %bitcast.7, s32[1,128]{1,0:T(1,128)} %bitcast.9, s32[3,128]{1,0:T(4,128)} %bitcast.8, s32[1,128]{1,0:T(1,128)} %bitcast.10, ...), custom_call_target="tpu_custom_call" | custom-call | flops 20000000000 | bytes 262144 | tf_op jit(solution)/shard_map/prep/pallas_call | solution.py:146
  2.0 0.0 copy-start.1
  2.1 14.9 %all_to_all.10.coef_ref = bf16[32,4,384]{2,1,0:T(4,128)(2,1)S(1)} all-to-all(bf16[32,4,384]{2,1,0:T(4,128)(2,1)S(1)} %get-tuple-element.7), channel_id=1, replica_groups=mesh['aux'=8,'lmo'=4] {'aux','lmo'}, dimensions={0} | all-to-all | bytes 196608 | tf_op jit(solution)/shard_map/all_to_all | solution.py:172
  17.0 0.0 copy-done
  17.0 3.4 %half_transform.1 = bf16[32,8,1024]{2,1,0:T(8,128)(2,1)S(1)} custom-call(bf16[8,768,768]{2,1,0:T(8,128)(2,1)S(1)} %copy-done, bf16[32,4,384]{2,1,0:T(4,128)(2,1)S(1)} %all_to_all.10.coef_ref, bf16[128,256]{1,0:T(8,128)(2,1)S(1)} %get-tuple-element.8.spread_ref, s32[8,256]{1,0:T(8,128)S(1)} %get-tuple-element.9.table_ref), custom_call_target="tpu_custom_call" | custom-call | flops 2415919104 | bytes 9437184 | tf_op jit(solution)/shard_map/half_transform/pallas_call | solution.py:173
  20.4 17.3 %all_to_all.11 = bf16[32,8,1024]{2,1,0:T(8,128)(2,1)S(1)} all-to-all(bf16[32,8,1024]{2,1,0:T(8,128)(2,1)S(1)} %half_transform.1), channel_id=1, replica_groups=mesh['aux'=8,'lmo'=4] {'aux','lmo'}, dimensions={0} | all-to-all | bytes 1048576 | tf_op jit(solution)/shard_map/all_to_all | solution.py:188
  37.7 0.0 copy-done.1
  37.7 2.4 %pair_transform.1 = (bf16[4,256,256]{2,1,0:T(8,128)(2,1)}, f32[4,256,256]{2,1,0:T(8,128)}) custom-call(s32[4,128]{1,0:T(4,128)S(1)} %get-tuple-element.6.counts_ref, bf16[256,1024]{1,0:T(8,128)(2,1)S(1)} %bitcast.6, bf16[4,384,256]{2,1,0:T(8,128)(2,1)S(1)} %copy-done.1), custom_call_target="tpu_custom_call" | custom-call | tf_op jit(solution)/shard_map/pair_transform/pallas_call | solution.py:193
Async XLA Ops:
  0.6 16.4 %copy-start = (bf16[8,768,768]{2,1,0:T(8,128)(2,1)S(1)}, bf16[8,768,768]{2,1,0:T(8,128)(2,1)}, u32[]{:S(2)}) copy-start(bf16[8,768,768]{2,1,0:T(8,128)(2,1)} %aux_ref.1) | copy-start | bytes 28311556
  2.0 35.7 %copy-start.1 = (bf16[4,384,256]{2,1,0:T(8,128)(2,1)S(1)}, bf16[4,384,256]{2,1,0:T(8,128)(2,1)}, u32[]{:S(2)}) copy-start(bf16[4,384,256]{2,1,0:T(8,128)(2,1)} %coef_ref.1) | copy-start | bytes 2359300

commit v4 on v3

--- a/solution.py
+++ b/solution.py
@@ -10,6 +10,26 @@
 PB = 3
 USED = 8
 AXES = ("aux", "lmo")
+
+GATHER_ORDER = (
+    10, 17, 31, 9, 5, 30, 29, 28, 24, 4, 15, 16, 18, 8, 25, 1, 0, 12, 6, 2, 3, 14, 13, 27, 22,
+    23, 19, 20, 11, 21, 26, 7,
+)
+SEND_ORDER = (
+    24, 27, 5, 30, 1, 19, 25, 2, 12, 18, 14, 6, 7, 9, 22, 8, 4, 11, 3, 20, 0, 21, 10, 29, 26,
+    16, 28, 23, 31, 13, 17, 15,
+)
+
+
+def participants(order, devices):
+    rank = {device: place for place, device in enumerate(order)}
+    return sorted(range(devices), key=lambda device: (rank[device % len(order)], device))
+
+
+def exchange(blocks, order):
+    return lax.all_to_all(
+        blocks, AXES, split_axis=0, concat_axis=0, tiled=True, axis_index_groups=[order]
+    )
 
 
 def prep_kernel(
@@ -70,15 +90,15 @@
         counts_ref[r : r + 1, :] = jnp.broadcast_to(count, (1, 128)).astype(jnp.int32)
 
 
-def half_kernel(aux_ref, coef_ref, spread_ref, table_ref, send_ref, flat_ref, tiles_ref):
-    sources, rows_each, _ = coef_ref.shape
+def half_kernel(gather_order, send_order, aux_ref, coef_ref, spread_ref, table_ref, send_ref, flat_ref, tiles_ref):
+    rows_each = coef_ref.shape[1]
     lmo_total, cols = spread_ref.shape
     devices, row_total, width = send_ref.shape
     used = width // BLK
     blocks = aux_ref.shape[1] // BLK
 
-    for src in range(sources):
-        flat_ref[pl.ds(src * rows_each, rows_each), :] = coef_ref[src].astype(jnp.float32)
+    for place, src in enumerate(gather_order):
+        flat_ref[pl.ds(src * rows_each, rows_each), :] = coef_ref[place].astype(jnp.float32)
     coef_t = flat_ref[...].T
     dense = []
     for b in range(blocks):
@@ -98,17 +118,19 @@
         picked = half[:BLK]
         for b in range(1, blocks):
             picked = jnp.where(block_row == b, half[b * BLK : (b + 1) * BLK], picked)
-        tiles_ref[:, p, :] = picked.T
-    for col in range(cols):
-        dev, slot = divmod(col, used)
-        send_ref[dev, :, slot * BLK : (slot + 1) * BLK] = tiles_ref[col].astype(jnp.bfloat16)
-
-
-def pair_kernel(counts_ref, rows_ref, coef_ref, pair_hbm, metric_hbm, pair_ref, metric_ref, sems):
+        tiles_ref[pl.ds(p, cols, stride=row_total), :] = picked.T
+    for place, dev in enumerate(send_order):
+        for slot in range(used):
+            tile = tiles_ref[pl.ds((dev * used + slot) * row_total, row_total), :]
+            send_ref[place, :, slot * BLK : (slot + 1) * BLK] = tile.astype(jnp.bfloat16)
+
+
+def pair_kernel(send_order, counts_ref, rows_ref, coef_ref, pair_hbm, metric_hbm, pair_ref, metric_ref, sems):
     owned, aux_total, _ = pair_ref.shape
     used = rows_ref.shape[1] // BLK
+    row_total = aux_total // len(send_order)
+    places = sorted(range(len(send_order)), key=lambda place: send_order[place])
     counts = [counts_ref[r : r + 1, :][0, 0] for r in range(owned)]
-    copies = []
     slot = 0
     for r in range(owned):
         parts = []
@@ -118,16 +140,23 @@
             parts.append(jnp.where(counts[r] > k, part, jnp.zeros_like(part)))
         slot = slot + counts[r]
         rows = jnp.concatenate(parts, axis=1)
-        pair = jnp.dot(rows, coef_ref[r], preferred_element_type=jnp.float32).astype(jnp.bfloat16)
-        pair_ref[r] = pair
-        copies.append(pltpu.make_async_copy(pair_ref.at[r], pair_hbm.at[r], sems.at[0, r]))
-        copies[-1].start()
+        pair = jnp.dot(rows, coef_ref[r], preferred_element_type=jnp.float32)
+        groups = [pair[place * row_total : (place + 1) * row_total] for place in places]
+        pair_ref[r] = jnp.concatenate(groups, axis=0).astype(jnp.bfloat16)
+    copies = [pltpu.make_async_copy(pair_ref, pair_hbm, sems.at[0])]
+    copies[0].start()
+    for r in range(owned):
+        pair = pair_ref[r]
         metric = lax.dot_general(
             pair, pair, (((0,), (0,)), ((), ())), preferred_element_type=jnp.float32
         )
         metric_ref[r] = metric / aux_total
-        copies.append(pltpu.make_async_copy(metric_ref.at[r], metric_hbm.at[r], sems.at[1, r]))
-        copies[-1].start()
+        if r % 1 == 0:
+            some = pl.ds(r - 0, 1)
+            copies.append(
+                pltpu.make_async_copy(metric_ref.at[some], metric_hbm.at[some], sems.at[1 + r // 1])
+            )
+            copies[-1].start()
     for copy in copies:
         copy.wait()
 
@@ -169,15 +198,17 @@
         pltpu.with_memory_space_constraint(x, pltpu.HBM)
         for x in (lmo_coef, ao_domain.T, ao_count[None], pao_domain.T, pao_count[None], owner_order[None])
     ))
-    coef = lax.all_to_all(bcast, AXES, split_axis=0, concat_axis=0, tiled=True)
+    gather_order = participants(GATHER_ORDER, devices)
+    send_order = participants(SEND_ORDER, devices)
+    coef = exchange(bcast, gather_order)
     send = pl.pallas_call(
-        half_kernel,
+        lambda *refs: half_kernel(gather_order, send_order, *refs),
         out_shape=jax.ShapeDtypeStruct((devices, row_total, USED * BLK), jnp.bfloat16),
         in_specs=[vmem] * 4,
         out_specs=vmem,
         scratch_shapes=[
             pltpu.VMEM((lmo_total, DB * BLK), jnp.float32),
-            pltpu.VMEM((cols, row_total, BLK), jnp.float32),
+            pltpu.VMEM((cols * row_total, BLK), jnp.float32),
         ],
         compiler_params=pltpu.CompilerParams(vmem_limit_bytes=24 * 2**20),
         cost_estimate=pl.CostEstimate(
@@ -185,17 +216,17 @@
         ),
         name="half_transform",
     )(aux_ints, coef, spread, table)
-    received = lax.all_to_all(send, AXES, split_axis=0, concat_axis=0, tiled=True)
+    received = exchange(send, send_order)
     outs = (
         ((owned, aux_total, pao_coef.shape[2]), jnp.bfloat16),
         ((owned, pao_coef.shape[2], pao_coef.shape[2]), jnp.float32),
     )
     return pl.pallas_call(
-        pair_kernel,
+        lambda *refs: pair_kernel(send_order, *refs),
         out_shape=tuple(jax.ShapeDtypeStruct(*out) for out in outs),
         in_specs=[vmem] * 3,
         out_specs=(pl.BlockSpec(memory_space=pltpu.HBM),) * 2,
-        scratch_shapes=[pltpu.VMEM(*out) for out in outs] + [pltpu.SemaphoreType.DMA((2, owned))],
+        scratch_shapes=[pltpu.VMEM(*out) for out in outs] + [pltpu.SemaphoreType.DMA((1 + owned // 1,))],
         compiler_params=small,
         name="pair_transform",
     )(counts, received.reshape(aux_total, USED * BLK), pao_coef)

time: 40.3 us -> 37.2 us (0.923)
  the two profiles are of different devices: /device:TPU:0 before, /device:TPU:5 now
where the time goes in v4:
time: 37.2 us; the launch traced here: 37.1 us
  blocking collectives  30.2 us (81%)
  Pallas kernels  6.18 us (17%)
  between operations  0.67 us (2%)
    all_to_all x2, blocking collectives, exchange(): lax.all_to_all(blocks, AXES, split_axis=0, concat_axis=0, tiled=True, axi...  30.2 us
    pallas_call x1, Pallas kernels, shards(): pl.pallas_call(lambda *refs: half_kernel(gather_order, send_order, *refs)...  3.12 us
    pallas_call x1, Pallas kernels, shards(): pl.pallas_call(lambda *refs: pair_kernel(send_order, *refs), out_shape=tu...  1.66 us
    pallas_call x1, Pallas kernels, shards(): pl.pallas_call(lambda *refs: prep_kernel(owned, USED, *refs), out_shape=(...  1.4 us

profile of v4, /device:TPU:5, one launch (start us, length us, event | category | flops | bytes accessed | tf_op | source)
XLA Modules:
  0.0 37.1 jit_solution(10954904403879671388)
XLA Ops:
  0.6 0.0 copy-start
  0.6 1.4 %prep.1 = (bf16[32,4,384]{2,1,0:T(4,128)(2,1)S(1)}, bf16[128,256]{1,0:T(8,128)(2,1)S(1)}, s32[8,256]{1,0:T(8,128)S(1)}, s32[4,128]{1,0:T(4,128)S(1)}) custom-call(bf16[4,384]{1,0:T(4,128)(2,1)} %refs_0_.2, s32[3,128]{1,0:T(4,128)} %bitcast.7, s32[1,128]{1,0:T(1,128)} %bitcast.9, s32[3,128]{1,0:T(4,128)} %bitcast.8, s32[1,128]{1,0:T(1,128)} %bitcast.10, ...), custom_call_target="tpu_custom_call" | custom-call | flops 20000000000 | bytes 262144 | tf_op jit(solution)/shard_map/prep/pallas_call | solution.py:175
  2.0 0.0 copy-start.1
  2.1 12.6 %all_to_all.10.refs_1_ = bf16[32,4,384]{2,1,0:T(4,128)(2,1)S(1)} all-to-all(bf16[32,4,384]{2,1,0:T(4,128)(2,1)S(1)} %get-tuple-element.7), channel_id=1, replica_groups={{10,17,31,9,5,30,29,28,24,4,15,16,18,8,25,1,0,12,6,2,3,14,13,27,22,23,1..., dimensions={0} | all-to-all | bytes 196608 | tf_op jit(solution)/shard_map/all_to_all | solution.py:30
  14.7 0.0 copy-done
  14.7 3.1 %half_transform.1 = bf16[32,8,1024]{2,1,0:T(8,128)(2,1)S(1)} custom-call(bf16[8,768,768]{2,1,0:T(8,128)(2,1)S(1)} %copy-done, bf16[32,4,384]{2,1,0:T(4,128)(2,1)S(1)} %all_to_all.10.refs_1_, bf16[128,256]{1,0:T(8,128)(2,1)S(1)} %get-tuple-element.8.refs_2_, s32[8,256]{1,0:T(8,128)S(1)} %get-tuple-element.9.refs_3_), custom_call_target="tpu_custom_call" | custom-call | flops 2415919104 | bytes 9437184 | tf_op jit(solution)/shard_map/half_transform/pallas_call | solution.py:204
  17.8 17.6 %all_to_all.11 = bf16[32,8,1024]{2,1,0:T(8,128)(2,1)S(1)} all-to-all(bf16[32,8,1024]{2,1,0:T(8,128)(2,1)S(1)} %half_transform.1), channel_id=1, replica_groups={{24,27,5,30,1,19,25,2,12,18,14,6,7,9,22,8,4,11,3,20,0,21,10,29,26,16,28..., dimensions={0} | all-to-all | bytes 1048576 | tf_op jit(solution)/shard_map/all_to_all | solution.py:30
  35.4 0.0 copy-done.1
  35.4 1.7 %pair_transform.1 = (bf16[4,256,256]{2,1,0:T(8,128)(2,1)}, f32[4,256,256]{2,1,0:T(8,128)}) custom-call(s32[4,128]{1,0:T(4,128)S(1)} %get-tuple-element.6.refs_0_, bf16[256,1024]{1,0:T(8,128)(2,1)S(1)} %bitcast.6, bf16[4,384,256]{2,1,0:T(8,128)(2,1)S(1)} %copy-done.1), custom_call_target="tpu_custom_call" | custom-call | tf_op jit(solution)/shard_map/pair_transform/pallas_call | solution.py:224
Async XLA Ops:
  0.6 14.1 %copy-start = (bf16[8,768,768]{2,1,0:T(8,128)(2,1)S(1)}, bf16[8,768,768]{2,1,0:T(8,128)(2,1)}, u32[]{:S(2)}) copy-start(bf16[8,768,768]{2,1,0:T(8,128)(2,1)} %refs_0_.3) | copy-start | bytes 28311556
  2.0 33.3 %copy-start.1 = (bf16[4,384,256]{2,1,0:T(8,128)(2,1)S(1)}, bf16[4,384,256]{2,1,0:T(8,128)(2,1)}, u32[]{:S(2)}) copy-start(bf16[4,384,256]{2,1,0:T(8,128)(2,1)} %refs_2_.1) | copy-start | bytes 2359300

commit v5 on v4

v5 whole, which is shorter than its diff:
```python
import jax
import jax.numpy as jnp
from jax import lax
from jax.experimental import pallas as pl
from jax.experimental.pallas import tpu as pltpu
from jax.sharding import PartitionSpec as P

BLK = 128
DB = 3
PB = 3
USED = 8
AXES = ("aux", "lmo")

GATHER_ORDER = (
    10, 17, 31, 9, 5, 30, 29, 28, 24, 4, 15, 16, 18, 8, 25, 1, 0, 12, 6, 2, 3, 14, 13, 27, 22,
    23, 19, 20, 11, 21, 26, 7,
)
SEND_ORDER = (
    24, 27, 5, 30, 1, 19, 25, 2, 12, 18, 14, 6, 7, 9, 22, 8, 4, 11, 3, 20, 0, 21, 10, 29, 26,
    16, 28, 23, 31, 13, 17, 15,
)


def participants(order, devices):
    rank = {device: place for place, device in enumerate(order)}
    return sorted(range(devices), key=lambda device: (rank[device % len(order)], device))


def exchange(blocks, order):
    return lax.all_to_all(
        blocks, AXES, split_axis=0, concat_axis=0, tiled=True, axis_index_groups=[order]
    )


def spread_kernel(coef_hbm, bcast_ref, coef_ref, sem):
    copy = pltpu.make_async_copy(coef_hbm, coef_ref, sem)
    copy.start()
    copy.wait()
    own = coef_ref[...]
    for dev in range(bcast_ref.shape[0]):
        bcast_ref[dev] = own


def rows_of(row, count):
    return jnp.broadcast_to(row, (count, row.shape[1])).astype(jnp.bfloat16)


def half_kernel(
    owned, gather_order, send_order,
    aux_ref, coef_ref, ao_dom_ref, ao_cnt_ref, pao_dom_ref, pao_cnt_ref, order_ref,
    send_ref, counts_ref, flat_ref, tiles_ref,
):
    rows_each = coef_ref.shape[1]
    lmo_total = order_ref.shape[1]
    devices, row_total, width = send_ref.shape
    used = width // BLK
    cols = devices * used
    blocks = aux_ref.shape[1] // BLK

    lmo_id = lax.broadcasted_iota(jnp.int32, (lmo_total, lmo_total), 0)
    held = jnp.where(order_ref[...] == lmo_id, 1.0, 0.0).astype(jnp.bfloat16)
    cnt_slot = jnp.dot(
        rows_of(pao_cnt_ref[...], 8), held, preferred_element_type=jnp.float32
    )[:1].astype(jnp.int32)
    slot_id = lax.broadcasted_iota(jnp.int32, (1, lmo_total), 1)
    member = slot_id % owned
    base = jnp.zeros_like(cnt_slot)
    for step in range(1, owned):
        base = base + jnp.where(member >= step, pltpu.roll(cnt_slot, step, 1), 0)
    facts = jnp.concatenate(
        [rows_of(fact, 128) for fact in (slot_id // owned, base, cnt_slot)], axis=0
    )
    facts = lax.dot_general(
        held, facts, (((1,), (1,)), ((), ())), preferred_element_type=jnp.float32
    ).astype(jnp.int32)
    first = facts[:, :128] * used + facts[:, 128:256]
    count = facts[:, 256:]

    lane = lax.broadcasted_iota(jnp.int32, (lmo_total, 128), 1)
    spread, block_row = [], []
    for part in range(cols // 128):
        hits = [
            jnp.where((first + k == lane + part * 128) & (count > k), 1.0, 0.0) for k in range(PB)
        ]
        spread.append(sum(hits).astype(jnp.bfloat16))
        block_row.append(
            sum(
                jnp.dot(
                    rows_of(pao_dom_ref[k : k + 1, :], 8),
                    hits[k].astype(jnp.bfloat16),
                    preferred_element_type=jnp.float32,
                )
                for k in range(PB)
            )[:1]
        )
    spread = jnp.concatenate(spread, axis=1)
    block_row = jnp.concatenate(block_row, axis=1)

    for place, src in enumerate(gather_order):
        flat_ref[pl.ds(src * rows_each, rows_each), :] = coef_ref[place].astype(jnp.float32)
    coef_t = flat_ref[...].T
    homes = [
        jnp.where(ao_cnt_ref[...] > k, ao_dom_ref[k : k + 1, :], -1) for k in range(DB)
    ]
    dense = []
    for b in range(blocks):
        total = jnp.zeros((BLK, lmo_total), jnp.float32)
        for k in range(DB):
            total = jnp.where(homes[k] == b, coef_t[k * BLK : (k + 1) * BLK, :], total)
        dense.append(total)
    dense_t = jnp.concatenate(dense, axis=0).astype(jnp.bfloat16)
    weights = jnp.dot(dense_t, spread, preferred_element_type=jnp.float32).astype(jnp.bfloat16)

    for p in range(row_total):
        half = jnp.dot(aux_ref[p], weights, preferred_element_type=jnp.float32)
        picked = half[:BLK]
        for b in range(1, blocks):
            picked = jnp.where(block_row == b, half[b * BLK : (b + 1) * BLK], picked)
        tiles_ref[pl.ds(p, cols, stride=row_total), :] = picked.T
    mine = lax.axis_index(AXES) * owned
    for r in range(owned):
        here = jnp.where(slot_id == mine + r, cnt_slot, 0).astype(jnp.float32)
        here = jnp.sum(here, axis=1, keepdims=True).astype(jnp.int32)
        counts_ref[r : r + 1, :] = jnp.broadcast_to(here, (1, 128))
    for place, dev in enumerate(send_order):
        for slot in range(used):
            tile = tiles_ref[pl.ds((dev * used + slot) * row_total, row_total), :]
            send_ref[place, :, slot * BLK : (slot + 1) * BLK] = tile.astype(jnp.bfloat16)


def pair_kernel(send_order, counts_ref, rows_ref, coef_ref, pair_hbm, metric_hbm, pair_ref, metric_ref, sems):
    owned, aux_total, _ = pair_ref.shape
    used = rows_ref.shape[1] // BLK
    row_total = aux_total // len(send_order)
    places = sorted(range(len(send_order)), key=lambda place: send_order[place])
    counts = [counts_ref[r : r + 1, :][0, 0] for r in range(owned)]
    copies = []
    slot = 0
    for r in range(owned):
        parts = []
        for k in range(PB):
            at = pl.multiple_of(jnp.minimum(slot + k, used - 1) * BLK, BLK)
            part = rows_ref[:, pl.ds(at, BLK)]
            parts.append(jnp.where(counts[r] > k, part, jnp.zeros_like(part)))
        slot = slot + counts[r]
        rows = jnp.concatenate(parts, axis=1)
        pair = jnp.dot(rows, coef_ref[r], preferred_element_type=jnp.float32)
        groups = [pair[place * row_total : (place + 1) * row_total] for place in places]
        pair_ref[r] = jnp.concatenate(groups, axis=0).astype(jnp.bfloat16)
        copies.append(pltpu.make_async_copy(pair_ref.at[r], pair_hbm.at[r], sems.at[owned + r]))
        copies[-1].start()
    for r in range(owned):
        pair = pair_ref[r]
        metric = lax.dot_general(
            pair, pair, (((0,), (0,)), ((), ())), preferred_element_type=jnp.float32
        )
        metric_ref[r] = metric / aux_total
        copies.append(pltpu.make_async_copy(metric_ref.at[r], metric_hbm.at[r], sems.at[r]))
        copies[-1].start()
    for copy in copies:
        copy.wait()


def shards(aux_ints, lmo_coef, ao_domain, ao_count, pao_domain, pao_count, owner_order, pao_coef):
    devices = lax.axis_size(AXES)
    rows_each = lmo_coef.shape[0]
    lmo_total = devices * rows_each
    row_total, ao_total, _ = aux_ints.shape
    owned = pao_coef.shape[0]
    aux_total = devices * row_total
    cols = devices * USED

    vmem = pl.BlockSpec(memory_space=pltpu.VMEM)
    small = pltpu.CompilerParams(vmem_limit_bytes=16 * 2**20)
    bcast = pl.pallas_call(
        spread_kernel,
        out_shape=jax.ShapeDtypeStruct((devices,) + lmo_coef.shape, jnp.bfloat16),
        in_specs=[pl.BlockSpec(memory_space=pltpu.HBM)],
        out_specs=vmem,
        scratch_shapes=[pltpu.VMEM(lmo_coef.shape, jnp.bfloat16), pltpu.SemaphoreType.DMA],
        compiler_params=small,
        cost_estimate=pl.CostEstimate(flops=2 * 10**10, bytes_accessed=2**18, transcendentals=0),
        name="spread",
    )(pltpu.with_memory_space_constraint(lmo_coef, pltpu.HBM))
    gather_order = participants(GATHER_ORDER, devices)
    send_order = participants(SEND_ORDER, devices)
    coef = exchange(bcast, gather_order)
    send, counts = pl.pallas_call(
        lambda *refs: half_kernel(owned, gather_order, send_order, *refs),
        out_shape=(
            jax.ShapeDtypeStruct((devices, row_total, USED * BLK), jnp.bfloat16),
            jax.ShapeDtypeStruct((owned, 128), jnp.int32),
        ),
        in_specs=[vmem] * 7,
        out_specs=(vmem,) * 2,
        scratch_shapes=[
            pltpu.VMEM((lmo_total, DB * BLK), jnp.float32),
            pltpu.VMEM((cols * row_total, BLK), jnp.float32),
        ],
        compiler_params=pltpu.CompilerParams(vmem_limit_bytes=24 * 2**20),
        cost_estimate=pl.CostEstimate(
            flops=2 * row_total * ao_total * ao_total * cols, bytes_accessed=2 * aux_ints.size, transcendentals=0
        ),
        name="half_transform",
    )(aux_ints, coef, ao_domain.T, ao_count[None], pao_domain.T, pao_count[None], owner_order[None])
    received = exchange(send, send_order)
    outs = (
        ((owned, aux_total, pao_coef.shape[2]), jnp.bfloat16),
        ((owned, pao_coef.shape[2], pao_coef.shape[2]), jnp.float32),
    )
    return pl.pallas_call(
        lambda *refs: pair_kernel(send_order, *refs),
        out_shape=tuple(jax.ShapeDtypeStruct(*out) for out in outs),
        in_specs=[vmem] * 3,
        out_specs=(pl.BlockSpec(memory_space=pltpu.HBM),) * 2,
        scratch_shapes=[pltpu.VMEM(*out) for out in outs] + [pltpu.SemaphoreType.DMA((2 * owned,))],
        compiler_params=small,
        name="pair_transform",
    )(counts, received.reshape(aux_total, USED * BLK), pao_coef)


def solution(mesh):
    placed = (
        P(AXES, None, None),
        P(AXES, None),
        P(),
        P(),
        P(),
        P(),
        P(),
        P(AXES, None, None),
    )
    return jax.shard_map(
        shards,
        mesh=mesh,
        in_specs=placed,
        out_specs=(P(AXES, None, None), P(AXES, None, None)),
        check_vma=False,
    )
```

time: 37.2 us -> 37.1 us (level)
  no operation moved by 1% of the time
where the time goes in v5:
time: 37.1 us; the launch traced here: 36.9 us
  blocking collectives  30.2 us (81%)
  Pallas kernels  5.9 us (16%)
  between operations  0.73 us (2%)
    all_to_all x2, blocking collectives, exchange(): lax.all_to_all(blocks, AXES, split_axis=0, concat_axis=0, tiled=True, axi...  30.2 us
    pallas_call x1, Pallas kernels, shards(): pl.pallas_call(lambda *refs: half_kernel(owned, gather_order, send_order,...  3.43 us
    pallas_call x1, Pallas kernels, shards(): pl.pallas_call(lambda *refs: pair_kernel(send_order, *refs), out_shape=tu...  1.62 us
    pallas_call x1, Pallas kernels, shards(): pl.pallas_call(spread_kernel, out_shape=jax.ShapeDtypeStruct((devices,) +...  0.85 us

profile of v5, /device:TPU:5, one launch (start us, length us, event | category | flops | bytes accessed | tf_op | source)
XLA Modules:
  0.0 36.9 jit_solution(6080723559971103250)
XLA Ops:
  0.6 0.0 copy-start.6
  0.6 0.0 copy-start.5
  0.7 0.0 copy-start.3
  0.7 0.0 copy-start.4
  0.7 0.0 copy-start.2
  0.7 0.0 copy-start
  0.7 0.9 %spread.1 = bf16[32,4,384]{2,1,0:T(4,128)(2,1)S(1)} custom-call(bf16[4,384]{1,0:T(4,128)(2,1)} %coef_hbm.1), custom_call_target="tpu_custom_call" | custom-call | flops 20000000000 | bytes 262144 | tf_op jit(solution)/shard_map/spread/pallas_call | solution.py:175
  1.6 0.0 copy-start.1
  1.6 12.6 %all_to_all.10.refs_1_ = bf16[32,4,384]{2,1,0:T(4,128)(2,1)S(1)} all-to-all(bf16[32,4,384]{2,1,0:T(4,128)(2,1)S(1)} %spread.1), channel_id=1, replica_groups={{10,17,31,9,5,30,29,28,24,4,15,16,18,8,25,1,0,12,6,2,3,14,13,27,22,23,1..., dimensions={0} | all-to-all | bytes 196608 | tf_op jit(solution)/shard_map/all_to_all | solution.py:30
  14.2 0.0 copy-done.6
  14.2 0.0 copy-done.5
  14.2 0.0 copy-done.3
  14.2 0.0 copy-done.4
  14.2 0.0 copy-done.2
  14.2 0.0 copy-done
  14.2 3.4 %half_transform.1 = (bf16[32,8,1024]{2,1,0:T(8,128)(2,1)S(1)}, s32[4,128]{1,0:T(4,128)S(1)}) custom-call(bf16[8,768,768]{2,1,0:T(8,128)(2,1)S(1)} %copy-done, bf16[32,4,384]{2,1,0:T(4,128)(2,1)S(1)} %all_to_all.10.refs_1_, s32[3,128]{1,0:T(4,128)S(1)} %bitcast.7, s32[1,128]{1,0:T(1,128)S(1)} %bitcast.9, s32[3,128]{1,0:T(4,128)S(1)} %bitcast.8, ...), custom_call_target="tpu_custom_call" | custom-call | flops 2415919104 | bytes 9437184 | tf_op jit(solution)/shard_map/half_transform/pallas_call | solution.py:188
  17.7 17.6 %all_to_all.11 = bf16[32,8,1024]{2,1,0:T(8,128)(2,1)S(1)} all-to-all(bf16[32,8,1024]{2,1,0:T(8,128)(2,1)S(1)} %get-tuple-element.5), channel_id=1, replica_groups={{24,27,5,30,1,19,25,2,12,18,14,6,7,9,22,8,4,11,3,20,0,21,10,29,26,16,28..., dimensions={0} | all-to-all | bytes 1048576 | tf_op jit(solution)/shard_map/all_to_all | solution.py:30
  35.2 0.0 copy-done.1
  35.2 1.6 %pair_transform.1 = (bf16[4,256,256]{2,1,0:T(8,128)(2,1)}, f32[4,256,256]{2,1,0:T(8,128)}) custom-call(s32[4,128]{1,0:T(4,128)S(1)} %get-tuple-element.4.refs_0_, bf16[256,1024]{1,0:T(8,128)(2,1)S(1)} %bitcast.6, bf16[4,384,256]{2,1,0:T(8,128)(2,1)S(1)} %copy-done.1), custom_call_target="tpu_custom_call" | custom-call | tf_op jit(solution)/shard_map/pair_transform/pallas_call | solution.py:211
Async XLA Ops:
  0.6 13.6 %copy-start.6 = (s32[128]{0:T(128)S(1)}, s32[128]{0:T(128)}, u32[]{:S(2)}) copy-start(s32[128]{0:T(128)} %param.14) | copy-start | bytes 1540
  0.6 13.6 %copy-start.5 = (s32[128]{0:T(128)S(1)}, s32[128]{0:T(128)}, u32[]{:S(2)}) copy-start(s32[128]{0:T(128)} %param.13) | copy-start | bytes 1540
  0.7 13.6 %copy-start.3 = (s32[128,3]{0,1:T(4,128)S(1)}, s32[128,3]{0,1:T(4,128)}, u32[]{:S(2)}) copy-start(s32[128,3]{0,1:T(4,128)} %param.12) | copy-start | bytes 4612
  0.7 13.6 %copy-start.4 = (s32[128]{0:T(128)S(1)}, s32[128]{0:T(128)}, u32[]{:S(2)}) copy-start(s32[128]{0:T(128)} %param.11) | copy-start | bytes 1540
  0.7 13.6 %copy-start.2 = (s32[128,3]{0,1:T(4,128)S(1)}, s32[128,3]{0,1:T(4,128)}, u32[]{:S(2)}) copy-start(s32[128,3]{0,1:T(4,128)} %param.10) | copy-start | bytes 4612
  0.7 13.6 %copy-start = (bf16[8,768,768]{2,1,0:T(8,128)(2,1)S(1)}, bf16[8,768,768]{2,1,0:T(8,128)(2,1)}, u32[]{:S(2)}) copy-start(bf16[8,768,768]{2,1,0:T(8,128)(2,1)} %refs_0_.1) | copy-start | bytes 28311556
  1.6 33.7 %copy-start.1 = (bf16[4,384,256]{2,1,0:T(8,128)(2,1)S(1)}, bf16[4,384,256]{2,1,0:T(8,128)(2,1)}, u32[]{:S(2)}) copy-start(bf16[4,384,256]{2,1,0:T(8,128)(2,1)} %refs_2_.1) | copy-start | bytes 2359300

commit v6 on v5

--- a/solution.py
+++ b/solution.py
@@ -12,12 +12,12 @@
 AXES = ("aux", "lmo")
 
 GATHER_ORDER = (
-    10, 17, 31, 9, 5, 30, 29, 28, 24, 4, 15, 16, 18, 8, 25, 1, 0, 12, 6, 2, 3, 14, 13, 27, 22,
-    23, 19, 20, 11, 21, 26, 7,
+    11, 0, 25, 21, 31, 22, 5, 20, 14, 30, 13, 16, 9, 7, 17, 1, 15, 12, 4, 2, 10, 3, 18, 19,
+    27, 24, 29, 6, 8, 28, 26, 23,
 )
 SEND_ORDER = (
-    24, 27, 5, 30, 1, 19, 25, 2, 12, 18, 14, 6, 7, 9, 22, 8, 4, 11, 3, 20, 0, 21, 10, 29, 26,
-    16, 28, 23, 31, 13, 17, 15,
+    24, 27, 5, 30, 1, 19, 25, 26, 16, 2, 12, 18, 14, 6, 7, 9, 22, 8, 4, 11, 3, 20, 0, 21, 10,
+    29, 28, 23, 31, 13, 17, 15,
 )
 
 
@@ -77,24 +77,26 @@
     count = facts[:, 256:]
 
     lane = lax.broadcasted_iota(jnp.int32, (lmo_total, 128), 1)
-    spread, block_row = [], []
+    spread = []
     for part in range(cols // 128):
-        hits = [
-            jnp.where((first + k == lane + part * 128) & (count > k), 1.0, 0.0) for k in range(PB)
-        ]
-        spread.append(sum(hits).astype(jnp.bfloat16))
-        block_row.append(
-            sum(
-                jnp.dot(
-                    rows_of(pao_dom_ref[k : k + 1, :], 8),
-                    hits[k].astype(jnp.bfloat16),
-                    preferred_element_type=jnp.float32,
-                )
-                for k in range(PB)
-            )[:1]
-        )
-    spread = jnp.concatenate(spread, axis=1)
-    block_row = jnp.concatenate(block_row, axis=1)
+        place = lane + part * 128 - first
+        spread.append(jnp.where((place >= 0) & (place < count), 1.0, 0.0))
+    spread = jnp.concatenate(spread, axis=1).astype(jnp.bfloat16)
+
+    by_lmo = lax.dot_general(
+        jnp.concatenate([rows_of(fact, 16) for fact in (slot_id // owned, base)], axis=0),
+        held, (((1,), (1,)), ((), ())), preferred_element_type=jnp.float32,
+    ).astype(jnp.bfloat16)
+    by_lmo = jnp.concatenate(
+        [by_lmo] + [rows_of(pao_dom_ref[k : k + 1, :], 16) for k in range(PB)], axis=0
+    )
+    by_col = jnp.dot(by_lmo, spread, preferred_element_type=jnp.float32)
+    by_col = [by_col[16 * n : 16 * n + 1] for n in range(2 + PB)]
+    col_id = lax.broadcasted_iota(jnp.int32, (1, cols), 1).astype(jnp.float32)
+    place = col_id - (by_col[0] * used + by_col[1])
+    block_row = by_col[2]
+    for k in range(1, PB):
+        block_row = jnp.where(place >= k, by_col[2 + k], block_row)
 
     for place, src in enumerate(gather_order):
         flat_ref[pl.ds(src * rows_each, rows_each), :] = coef_ref[place].astype(jnp.float32)

time: 37.1 us -> 36.8 us (level); the launches traced: 36.9 us -> 36.1 us
  blocking collectives: 30.2 us -> 29.5 us
    all_to_all x2, blocking collectives: 30.2 us -> 29.5 us  [exchange(): lax.all_to_all(blocks, AXES, split_axis=0, concat_axis=0, tiled=True, axi...]
where the time goes in v6:
time: 36.8 us; the launch traced here: 36.1 us
  blocking collectives  29.5 us (80%)
  Pallas kernels  5.86 us (16%)
  between operations  0.73 us (2%)
    all_to_all x2, blocking collectives, exchange(): lax.all_to_all(blocks, AXES, split_axis=0, concat_axis=0, tiled=True, axi...  29.5 us
    pallas_call x1, Pallas kernels, shards(): pl.pallas_call(lambda *refs: half_kernel(owned, gather_order, send_order,...  3.38 us
    pallas_call x1, Pallas kernels, shards(): pl.pallas_call(lambda *refs: pair_kernel(send_order, *refs), out_shape=tu...  1.63 us
    pallas_call x1, Pallas kernels, shards(): pl.pallas_call(spread_kernel, out_shape=jax.ShapeDtypeStruct((devices,) +...  0.85 us

profile of v6, /device:TPU:5, one launch (start us, length us, event | category | flops | bytes accessed | tf_op | source)
XLA Modules:
  0.0 36.1 jit_solution(13175380132545247261)
XLA Ops:
  0.6 0.0 copy-start.6
  0.6 0.0 copy-start.5
  0.7 0.0 copy-start.3
  0.7 0.0 copy-start.4
  0.7 0.0 copy-start.2
  0.7 0.0 copy-start
  0.7 0.9 %spread.1 = bf16[32,4,384]{2,1,0:T(4,128)(2,1)S(1)} custom-call(bf16[4,384]{1,0:T(4,128)(2,1)} %coef_hbm.1), custom_call_target="tpu_custom_call" | custom-call | flops 20000000000 | bytes 262144 | tf_op jit(solution)/shard_map/spread/pallas_call | solution.py:177
  1.6 0.0 copy-start.1
  1.6 12.5 %all_to_all.10.refs_1_ = bf16[32,4,384]{2,1,0:T(4,128)(2,1)S(1)} all-to-all(bf16[32,4,384]{2,1,0:T(4,128)(2,1)S(1)} %spread.1), channel_id=1, replica_groups={{11,0,25,21,31,22,5,20,14,30,13,16,9,7,17,1,15,12,4,2,10,3,18,19,27,24,..., dimensions={0} | all-to-all | bytes 196608 | tf_op jit(solution)/shard_map/all_to_all | solution.py:30
  14.1 0.0 copy-done.6
  14.1 0.0 copy-done.5
  14.1 0.0 copy-done.3
  14.1 0.0 copy-done.4
  14.1 0.0 copy-done.2
  14.1 0.0 copy-done
  14.1 3.4 %half_transform.1 = (bf16[32,8,1024]{2,1,0:T(8,128)(2,1)S(1)}, s32[4,128]{1,0:T(4,128)S(1)}) custom-call(bf16[8,768,768]{2,1,0:T(8,128)(2,1)S(1)} %copy-done, bf16[32,4,384]{2,1,0:T(4,128)(2,1)S(1)} %all_to_all.10.refs_1_, s32[3,128]{1,0:T(4,128)S(1)} %bitcast.7, s32[1,128]{1,0:T(1,128)S(1)} %bitcast.9, s32[3,128]{1,0:T(4,128)S(1)} %bitcast.8, ...), custom_call_target="tpu_custom_call" | custom-call | flops 2415919104 | bytes 9437184 | tf_op jit(solution)/shard_map/half_transform/pallas_call | solution.py:190
  17.5 17.0 %all_to_all.11 = bf16[32,8,1024]{2,1,0:T(8,128)(2,1)S(1)} all-to-all(bf16[32,8,1024]{2,1,0:T(8,128)(2,1)S(1)} %get-tuple-element.5), channel_id=1, replica_groups={{24,27,5,30,1,19,25,26,16,2,12,18,14,6,7,9,22,8,4,11,3,20,0,21,10,29,28..., dimensions={0} | all-to-all | bytes 1048576 | tf_op jit(solution)/shard_map/all_to_all | solution.py:30
  34.5 0.0 copy-done.1
  34.5 1.6 %pair_transform.1 = (bf16[4,256,256]{2,1,0:T(8,128)(2,1)}, f32[4,256,256]{2,1,0:T(8,128)}) custom-call(s32[4,128]{1,0:T(4,128)S(1)} %get-tuple-element.4.refs_0_, bf16[256,1024]{1,0:T(8,128)(2,1)S(1)} %bitcast.6, bf16[4,384,256]{2,1,0:T(8,128)(2,1)S(1)} %copy-done.1), custom_call_target="tpu_custom_call" | custom-call | tf_op jit(solution)/shard_map/pair_transform/pallas_call | solution.py:213
Async XLA Ops:
  0.6 13.4 %copy-start.6 = (s32[128]{0:T(128)S(1)}, s32[128]{0:T(128)}, u32[]{:S(2)}) copy-start(s32[128]{0:T(128)} %param.14) | copy-start | bytes 1540
  0.6 13.4 %copy-start.5 = (s32[128]{0:T(128)S(1)}, s32[128]{0:T(128)}, u32[]{:S(2)}) copy-start(s32[128]{0:T(128)} %param.13) | copy-start | bytes 1540
  0.7 13.4 %copy-start.3 = (s32[128,3]{0,1:T(4,128)S(1)}, s32[128,3]{0,1:T(4,128)}, u32[]{:S(2)}) copy-start(s32[128,3]{0,1:T(4,128)} %param.12) | copy-start | bytes 4612
  0.7 13.4 %copy-start.4 = (s32[128]{0:T(128)S(1)}, s32[128]{0:T(128)}, u32[]{:S(2)}) copy-start(s32[128]{0:T(128)} %param.11) | copy-start | bytes 1540
  0.7 13.4 %copy-start.2 = (s32[128,3]{0,1:T(4,128)S(1)}, s32[128,3]{0,1:T(4,128)}, u32[]{:S(2)}) copy-start(s32[128,3]{0,1:T(4,128)} %param.10) | copy-start | bytes 4612
  0.7 13.4 %copy-start = (bf16[8,768,768]{2,1,0:T(8,128)(2,1)S(1)}, bf16[8,768,768]{2,1,0:T(8,128)(2,1)}, u32[]{:S(2)}) copy-start(bf16[8,768,768]{2,1,0:T(8,128)(2,1)} %refs_0_.1) | copy-start | bytes 28311556
  1.6 32.9 %copy-start.1 = (bf16[4,384,256]{2,1,0:T(8,128)(2,1)S(1)}, bf16[4,384,256]{2,1,0:T(8,128)(2,1)}, u32[]{:S(2)}) copy-start(bf16[4,384,256]{2,1,0:T(8,128)(2,1)} %refs_2_.1) | copy-start | bytes 2359300

commit v7 on v6

--- a/solution.py
+++ b/solution.py
@@ -110,11 +110,22 @@
         for k in range(DB):
             total = jnp.where(homes[k] == b, coef_t[k * BLK : (k + 1) * BLK, :], total)
         dense.append(total)
-    dense_t = jnp.concatenate(dense, axis=0).astype(jnp.bfloat16)
-    weights = jnp.dot(dense_t, spread, preferred_element_type=jnp.float32).astype(jnp.bfloat16)
+    weights = []
+    for b in range(0, blocks, 2):
+        dense_t = jnp.concatenate(dense[b : b + 2], axis=0).astype(jnp.bfloat16)
+        weights.append(
+            jnp.dot(dense_t, spread, preferred_element_type=jnp.float32).astype(jnp.bfloat16)
+        )
 
     for p in range(row_total):
-        half = jnp.dot(aux_ref[p], weights, preferred_element_type=jnp.float32)
+        half = sum(
+            jnp.dot(
+                aux_ref[p, :, 2 * BLK * n : 2 * BLK * (n + 1)],
+                weight,
+                preferred_element_type=jnp.float32,
+            )
+            for n, weight in enumerate(weights)
+        )
         picked = half[:BLK]
         for b in range(1, blocks):
             picked = jnp.where(block_row == b, half[b * BLK : (b + 1) * BLK], picked)

time: 36.8 us -> 36.8 us (level)
  no operation moved by 1% of the time
where the time goes in v7:
time: 36.8 us; the launch traced here: 36.1 us
  blocking collectives  29.5 us (80%)
  Pallas kernels  5.89 us (16%)
  between operations  0.73 us (2%)
    all_to_all x2, blocking collectives, exchange(): lax.all_to_all(blocks, AXES, split_axis=0, concat_axis=0, tiled=True, axi...  29.5 us
    pallas_call x1, Pallas kernels, shards(): pl.pallas_call(lambda *refs: half_kernel(owned, gather_order, send_order,...  3.4 us
    pallas_call x1, Pallas kernels, shards(): pl.pallas_call(lambda *refs: pair_kernel(send_order, *refs), out_shape=tu...  1.63 us
    pallas_call x1, Pallas kernels, shards(): pl.pallas_call(spread_kernel, out_shape=jax.ShapeDtypeStruct((devices,) +...  0.85 us

profile of v7, /device:TPU:5, one launch (start us, length us, event | category | flops | bytes accessed | tf_op | source)
XLA Modules:
  0.0 36.1 jit_solution(17607923261009489387)
XLA Ops:
  0.6 0.0 copy-start.6
  0.6 0.0 copy-start.5
  0.7 0.0 copy-start.3
  0.7 0.0 copy-start.4
  0.7 0.0 copy-start.2
  0.7 0.0 copy-start
  0.7 0.9 %spread.1 = bf16[32,4,384]{2,1,0:T(4,128)(2,1)S(1)} custom-call(bf16[4,384]{1,0:T(4,128)(2,1)} %coef_hbm.1), custom_call_target="tpu_custom_call" | custom-call | flops 20000000000 | bytes 262144 | tf_op jit(solution)/shard_map/spread/pallas_call | solution.py:188
  1.6 0.0 copy-start.1
  1.6 12.5 %all_to_all.10.refs_1_ = bf16[32,4,384]{2,1,0:T(4,128)(2,1)S(1)} all-to-all(bf16[32,4,384]{2,1,0:T(4,128)(2,1)S(1)} %spread.1), channel_id=1, replica_groups={{11,0,25,21,31,22,5,20,14,30,13,16,9,7,17,1,15,12,4,2,10,3,18,19,27,24,..., dimensions={0} | all-to-all | bytes 196608 | tf_op jit(solution)/shard_map/all_to_all | solution.py:30
  14.1 0.0 copy-done.6
  14.1 0.0 copy-done.5
  14.1 0.0 copy-done.3
  14.1 0.0 copy-done.4
  14.1 0.0 copy-done.2
  14.1 0.0 copy-done
  14.1 3.4 %half_transform.1 = (bf16[32,8,1024]{2,1,0:T(8,128)(2,1)S(1)}, s32[4,128]{1,0:T(4,128)S(1)}) custom-call(bf16[8,768,768]{2,1,0:T(8,128)(2,1)S(1)} %copy-done, bf16[32,4,384]{2,1,0:T(4,128)(2,1)S(1)} %all_to_all.10.refs_1_, s32[3,128]{1,0:T(4,128)S(1)} %bitcast.7, s32[1,128]{1,0:T(1,128)S(1)} %bitcast.9, s32[3,128]{1,0:T(4,128)S(1)} %bitcast.8, ...), custom_call_target="tpu_custom_call" | custom-call | flops 2415919104 | bytes 9437184 | tf_op jit(solution)/shard_map/half_transform/pallas_call | solution.py:201
  17.5 17.0 %all_to_all.11 = bf16[32,8,1024]{2,1,0:T(8,128)(2,1)S(1)} all-to-all(bf16[32,8,1024]{2,1,0:T(8,128)(2,1)S(1)} %get-tuple-element.5), channel_id=1, replica_groups={{24,27,5,30,1,19,25,26,16,2,12,18,14,6,7,9,22,8,4,11,3,20,0,21,10,29,28..., dimensions={0} | all-to-all | bytes 1048576 | tf_op jit(solution)/shard_map/all_to_all | solution.py:30
  34.5 0.0 copy-done.1
  34.5 1.6 %pair_transform.1 = (bf16[4,256,256]{2,1,0:T(8,128)(2,1)}, f32[4,256,256]{2,1,0:T(8,128)}) custom-call(s32[4,128]{1,0:T(4,128)S(1)} %get-tuple-element.4.refs_0_, bf16[256,1024]{1,0:T(8,128)(2,1)S(1)} %bitcast.6, bf16[4,384,256]{2,1,0:T(8,128)(2,1)S(1)} %copy-done.1), custom_call_target="tpu_custom_call" | custom-call | tf_op jit(solution)/shard_map/pair_transform/pallas_call | solution.py:224
Async XLA Ops:
  0.6 13.4 %copy-start.6 = (s32[128]{0:T(128)S(1)}, s32[128]{0:T(128)}, u32[]{:S(2)}) copy-start(s32[128]{0:T(128)} %param.14) | copy-start | bytes 1540
  0.6 13.4 %copy-start.5 = (s32[128]{0:T(128)S(1)}, s32[128]{0:T(128)}, u32[]{:S(2)}) copy-start(s32[128]{0:T(128)} %param.13) | copy-start | bytes 1540
  0.7 13.4 %copy-start.3 = (s32[128,3]{0,1:T(4,128)S(1)}, s32[128,3]{0,1:T(4,128)}, u32[]{:S(2)}) copy-start(s32[128,3]{0,1:T(4,128)} %param.12) | copy-start | bytes 4612
  0.7 13.4 %copy-start.4 = (s32[128]{0:T(128)S(1)}, s32[128]{0:T(128)}, u32[]{:S(2)}) copy-start(s32[128]{0:T(128)} %param.11) | copy-start | bytes 1540
  0.7 13.4 %copy-start.2 = (s32[128,3]{0,1:T(4,128)S(1)}, s32[128,3]{0,1:T(4,128)}, u32[]{:S(2)}) copy-start(s32[128,3]{0,1:T(4,128)} %param.10) | copy-start | bytes 4612
  0.7 13.4 %copy-start = (bf16[8,768,768]{2,1,0:T(8,128)(2,1)S(1)}, bf16[8,768,768]{2,1,0:T(8,128)(2,1)}, u32[]{:S(2)}) copy-start(bf16[8,768,768]{2,1,0:T(8,128)(2,1)} %refs_0_.1) | copy-start | bytes 28311556
  1.6 33.0 %copy-start.1 = (bf16[4,384,256]{2,1,0:T(8,128)(2,1)S(1)}, bf16[4,384,256]{2,1,0:T(8,128)(2,1)}, u32[]{:S(2)}) copy-start(bf16[4,384,256]{2,1,0:T(8,128)(2,1)} %refs_2_.1) | copy-start | bytes 2359300
